TPU v7x, 128 devices: a whole 4x4x4 slice. The times are simulated.
128 devices in a mesh: scen: 32 (over x, y, core), own: 4 (over z).
Axes of the slice: x: 4, y: 4, z: 4, core: 2. Of those that a mesh axis runs over, the one named last changes fastest.
Arguments:
- returns: float32 [32768, 4096], P('scen', 'own'), may hold values from -50 to 50, as said below
Outputs:
- shrunk_cov: float32 [4096, 4096], P('scen', 'own')
Inputs may be any that keep to these rules, and one draw needn't show every extreme that they name: Finite real returns.
All inputs are finite; a program needn't handle non-finite values.
Results may differ from a plain program's by a relative error of at most 0.00014.
Values sent between devices are 32-bit elements; how exact they have to be, the bound alone decides.
No kernel may reach another device: no remote copies, remote signals or barrier semaphores. Data moves between devices by JAX's collectives and lax.ppermute only.
A program may use at most 128 MiB of HBM per device.

v0:
```python
import functools

import jax
import jax.numpy as jnp
from jax import lax
from jax.sharding import Mesh
from jax.sharding import PartitionSpec as P

SCEN = ("scen_0", "scen_1", "scen_2")
SCEN_OWN = ("scen_0", "scen_1", "scen_2", "own")


epsilon = 1e-06


def sent_to_all(array, axis):
    copies = jnp.broadcast_to(array, (lax.axis_size(axis), *array.shape))
    return lax.all_to_all(copies, axis, split_axis=0, concat_axis=0, tiled=True)


def over_copies(array, axis):
    everything = sent_to_all(array, axis)
    return jnp.sum(everything, axis=0)


def together(arrays, axis):
    ends = [0]
    for a in arrays:
        ends.append(ends[-1] + a.size)
    subtotal = over_copies(jnp.concatenate([a.ravel() for a in arrays]), axis)
    return tuple((subtotal[b:e].reshape(a.shape) for a, b, e in zip(arrays, ends, ends[1:])))


def by_axis(array, axes):
    return functools.reduce(lax.psum, axes, array)


def product_over_scenarios(left_part, right_part):
    return lax.dot_general(
        left_part,
        right_part,
        (((0,), (0,)), ((), ())),
        precision=lax.Precision.HIGHEST,
        preferred_element_type=jnp.float32,
    )


def on_device(returns):
    scen_devices = lax.axis_size(SCEN)
    own_devices = lax.axis_size("own")
    local_rows = returns.shape[0]
    own_cols = returns.shape[1]
    scenarios = local_rows * scen_devices
    order = own_cols * own_devices
    col_total = over_copies(jnp.sum(returns, axis=0), SCEN)
    centered = returns - col_total / scenarios
    wide_rows = lax.all_gather(centered, "own", axis=1, tiled=True)
    squares = wide_rows * wide_rows
    row_norm = jnp.sum(squares, axis=1)
    beta_local = jnp.sum(row_norm * row_norm)
    trace_sum, beta_raw = together((jnp.sum(squares), beta_local), SCEN)
    gram_tile = lax.psum_scatter(
        product_over_scenarios(wide_rows, centered), SCEN, scatter_dimension=0, tiled=True
    )
    covariance = gram_tile / scenarios
    frob_local = jnp.sum(covariance * covariance)
    frob_sum = by_axis(frob_local, SCEN_OWN)
    target = trace_sum / (scenarios * order)
    beta_term = (beta_raw / scenarios - frob_sum) / (order * scenarios)
    delta_term = (frob_sum - order * target * target) / order
    shrinkage = beta_term / (delta_term + epsilon)
    tile_height = covariance.shape[0]
    row_ids = lax.axis_index(SCEN) * tile_height + lax.broadcasted_iota(
        jnp.int32, covariance.shape, 0
    )
    col_ids = lax.axis_index("own") * own_cols + lax.broadcasted_iota(
        jnp.int32, covariance.shape, 1
    )
    diag_mask = (row_ids == col_ids).astype(jnp.float32)
    return (1.0 - shrinkage) * covariance + shrinkage * target * diag_mask


def solution(mesh):
    torus = Mesh(
        mesh.devices.reshape(4, 4, 2, mesh.shape["own"]), ("scen_0", "scen_1", "scen_2", "own")
    )
    in_specs = (P(SCEN, "own"),)
    out_specs = P(SCEN, "own")
    return jax.shard_map(
        on_device, mesh=torus, in_specs=in_specs, out_specs=out_specs, check_vma=False
    )
```

profile of v0, /device:TPU:0, one launch (start us, length us, event | category | flops | bytes accessed | tf_op | source)
XLA Modules:
  0.0 406.5 jit_solution(3477778867965493982)
XLA Ops:
  6.5 0.0 all-gather.2.cloned.1.call-start
  6.5 2.5 reduce_sum.63
  9.0 0.1 broadcast_in_dim.7
  9.1 15.1 %all_to_all.12 = f32[32,1,1024]{2,1,0:T(1,128)S(1)} all-to-all(f32[32,1,1024]{2,1,0:T(1,128)S(1)} %broadcast_in_dim.7), channel_id=1, replica_groups=mesh['scen_0'=4,'scen_1'=4,'scen_2'=2,'own'=4] {'scen_0','scen_1','scen_2'}, dimensions={0} | all-to-all | bytes 262144 | tf_op jit(solution)/shard_map/all_to_all | solution.py:18
  24.1 0.1 reduce_sum.64
  24.2 5.1 %broadcast_subtract_fusion = f32[1024,1024]{1,0:T(8,128)} fusion(f32[1024,1024]{1,0:T(8,128)} %param.1, f32[1024]{0:T(1024)S(1)} %broadcast_multiply_fusion), kind=kLoop, calls=%fused_computation.2 | loop fusion | flops 1048576 | bytes 8392704 | tf_op jit(solution)/shard_map/sub | solution.py:56
  29.3 0.0 all-gather.2.cloned.1.call-update
  29.4 0.0 reduce-scatter.2.cloned.1.call-start
  29.4 152.9 %all-gather.2.cloned.1.call-done = f32[1024,4096]{1,0:T(8,128)} async-done(((f32[1024,1024]{1,0:T(8,128)}), f32[1024,4096]{1,0:T(8,128)}) %all-gather.2.cloned.1.call-update) | async-done | bytes 16777232 | tf_op jit(solution)/shard_map/all_gather | solution.py:57
  182.3 59.2 %fusion.1 = f32[4096,1024]{1,0:T(8,128)} fusion(f32[1024,4096]{1,0:T(8,128)} %all-gather.2.cloned.1.call-done, f32[1024,1024]{1,0:T(8,128)} %broadcast_subtract_fusion), kind=kOutput, calls=%fused_computation.11 | convolution fusion | flops 51539607552 | bytes 37748736 | tf_op jit(solution)/shard_map/dot_general | solution.py:39
  241.5 0.0 reduce-scatter.2.cloned.1.call-update
  241.5 12.0 %multiply_reduce_fusion.1 = (f32[]{:T(128)}, f32[1024]{0:T(1024)S(1)}) fusion(f32[1024,4096]{1,0:T(8,128)} %all-gather.2.cloned.1.call-done), kind=kLoop, calls=%fused_computation.1 | loop fusion | flops 12581887 | bytes 16781316 | tf_op jit(solution)/shard_map/reduce_sum | solution.py:61
  253.5 0.6 multiply_reduce_fusion.3
  254.1 1.3 pad_maximum_fusion
  255.4 0.6 broadcast_in_dim.8
  256.0 7.1 %all-to-all-start.1 = ((f32[32,1,2]{2,1,0:T(1,128)}), f32[32,1,2]{2,1,0:T(1,128)S(1)}, u32[]{:S(2)}, u32[]{:S(2)}) async-start(f32[32,1,2]{2,1,0:T(1,128)} %broadcast_in_dim.8), calls=%async_computation.2 | async-start | bytes 32768 | tf_op jit(solution)/shard_map/all_to_all | solution.py:18
  263.1 7.3 %all-to-all-done.1 = f32[32,1,2]{2,1,0:T(1,128)S(1)} async-done(((f32[32,1,2]{2,1,0:T(1,128)}), f32[32,1,2]{2,1,0:T(1,128)S(1)}, u32[]{:S(2)}, u32[]{:S(2)}) %all-to-all-start.1) | async-done | bytes 288 | tf_op jit(solution)/shard_map/all_to_all | solution.py:18
  270.4 0.1 reduce_sum.68
  270.5 0.6 fusion
  271.1 86.8 %reduce-scatter.2.cloned.1.call-done = f32[128,1024]{1,0:T(8,128)} async-done(((f32[4096,1024]{1,0:T(8,128)}), f32[128,1024]{1,0:T(8,128)}) %reduce-scatter.2.cloned.1.call-update) | async-done | bytes 524304 | tf_op jit(solution)/shard_map/reduce_scatter | solution.py:62
  357.9 1.8 multiply_reduce_fusion.2
  361.0 10.8 %psum.28 = f32[]{:T(128)} all-reduce(f32[]{:T(128)} %multiply_reduce_fusion.2), channel_id=1, replica_groups=mesh['scen_0'=4,'scen_1'=4,'scen_2'=2,'own'=4] {'scen_0'}, use_global_device_ids=true, to_apply=%region_8.0 | all-reduce | flops 1 | bytes 8 | tf_op jit(solution)/shard_map/psum | solution.py:35
  372.4 9.0 %psum.29 = f32[]{:T(128)} all-reduce(f32[]{:T(128)} %psum.28), channel_id=1, replica_groups=mesh['scen_0'=4,'scen_1'=4,'scen_2'=2,'own'=4] {'scen_1'}, use_global_device_ids=true, to_apply=%region_9.0 | all-reduce | flops 1 | bytes 8 | tf_op jit(solution)/shard_map/psum | solution.py:35
  382.0 3.0 psum.30
  385.0 11.4 %psum.31 = f32[]{:T(128)} all-reduce(f32[]{:T(128)} %psum.30), channel_id=1, replica_groups=mesh['scen_0'=4,'scen_1'=4,'scen_2'=2,'own'=4] {'own'}, use_global_device_ids=true, to_apply=%region_11.0 | all-reduce | flops 1 | bytes 8 | tf_op jit(solution)/shard_map/psum | solution.py:35
  397.7 2.0 select_add_fusion
  (3 shorter events, 0.0 us)
Async XLA Ops:
  6.5 175.8 %all-gather.2.cloned.1.call-start = ((), (), s32[]{:S(2)}) async-start(), calls=%async_computation.3 | async-start | bytes 20971520 | tf_op jit(solution)/shard_map/all_gather | solution.py:57
  29.4 328.5 %reduce-scatter.2.cloned.1.call-start = ((), (), s32[]{:S(2)}) async-start(), calls=%async_computation.4 | async-start | bytes 17301504 | tf_op jit(solution)/shard_map/reduce_scatter | solution.py:62
  256.0 14.4 %all-to-all-start.1 = ((f32[32,1,2]{2,1,0:T(1,128)}), f32[32,1,2]{2,1,0:T(1,128)S(1)}, u32[]{:S(2)}, u32[]{:S(2)}) async-start(f32[32,1,2]{2,1,0:T(1,128)} %broadcast_in_dim.8), calls=%async_computation.2 | async-start | bytes 32768 | tf_op jit(solution)/shard_map/all_to_all | solution.py:18
Sparse Core Ops, SparseCore 0:
  29.5 152.7 all-gather.1
  241.6 116.1 reduce-scatter.1
where the time goes:
time: 407 us
  waiting for transfers between devices  247 us (61%)
  matrix products  59.2 us (15%)
  blocking collectives  49.3 us (12%)
  other arithmetic  25.3 us (6%)
  between operations  17.3 us (4%)
  starting transfers between devices  7.13 us (2%)
    all_gather x1, waiting for transfers between devices, on_device(): wide_rows = lax.all_gather(centered, 'own', axis=1, tiled=True)  153 us
    reduce_scatter x1, waiting for transfers between devices, on_device(): lax.psum_scatter(product_over_scenarios(wide_rows, centered), SCEN, scatt...  86.8 us
    dot_general x1, matrix products, product_over_scenarios(): lax.dot_general(left_part, right_part, (((0,), (0,)), ((), ())), precisio...  59.2 us
    psum x4, blocking collectives, by_axis(): return functools.reduce(lax.psum, axes, array)  34.2 us
    all_to_all x1, blocking collectives, sent_to_all(): return lax.all_to_all(copies, axis, split_axis=0, concat_axis=0, tiled=True)  15.1 us
    reduce_sum x1, other arithmetic, on_device(): trace_sum, beta_raw = together((jnp.sum(squares), beta_local), SCEN)  12 us
  transfers between devices with their start and end apart: 3, of which 3 were waited for; matrix products, arithmetic and copies ran while one was open for 4% of the time, Pallas kernels for 0%

commit v1 on v0

v1 whole, which is shorter than its diff:
```python
import functools

import jax
import jax.numpy as jnp
from jax import lax
from jax.experimental import pallas as pl
from jax.experimental.pallas import tpu as pltpu
from jax.sharding import Mesh
from jax.sharding import PartitionSpec as P


AXES = ("x", "y", "c", "z")
SCEN = ("x", "y", "c")
EPS = 1e-06
VMEM = 20 * 2**20


def routes(move):
    pairs = []
    for x in range(4):
        for y in range(4):
            for c in range(2):
                for z in range(4):
                    a, b, d, e = move(x, y, c, z)
                    pairs.append((((x * 4 + y) * 2 + c) * 4 + z, ((a * 4 + b) * 2 + d) * 4 + e % 4))
    return pairs


def side(c):
    return 1 if c == 0 else 3


TO_Z = routes(lambda x, y, c, z: (x, y, c, z - side(c)))
OTHER_CORE = routes(lambda x, y, c, z: (x, y, 1 - c, z))
FLIP_NEAR = [
    routes(lambda x, y, c, z, f=f: (y, x, c if f == 0 else 1 - c, z + side(c))) for f in (0, 1)
]
FLIP_FAR = [routes(lambda x, y, c, z, f=f: (y, x, c if f == 0 else 1 - c, z + 2)) for f in (0, 1)]
ACROSS = routes(lambda x, y, c, z: (x, y, c, z + 2))
X_BY = {d: routes(lambda x, y, c, z, d=d: (x ^ d, y, c, z)) for d in (1, 2, 3)}
X_HALF = [routes(lambda x, y, c, z, f=f: (x ^ (1 if c == f else 3), y, c, z)) for f in (0, 1)]
Y_HALF = [routes(lambda x, y, c, z, f=f: (x, y ^ (1 if c == f else 3), c, z)) for f in (0, 1)]


def send(a, route):
    return lax.ppermute(a, AXES, route)


def to_everyone(a, axes):
    copies = jnp.broadcast_to(a, (lax.axis_size(axes), *a.shape))
    return lax.all_to_all(copies, axes, split_axis=0, concat_axis=0, tiled=True)


def swapped(k):
    return jnp.where(k == 1, 2, jnp.where(k == 2, 1, k))


def high_low(a):
    high = a.astype(jnp.bfloat16)
    return high, (a - high.astype(jnp.float32)).astype(jnp.bfloat16)


def prepare_body(at_ref, a_ref, mean_ref, high_ref, low_ref):
    g = a_ref.shape[1] // 8
    for j in range(8):
        cols = pl.ds(pl.multiple_of(at_ref[j] * g, g), g)
        to = slice(j * g, (j + 1) * g)
        high_ref[:, to], low_ref[:, to] = high_low(a_ref[:, cols] - mean_ref[:, cols])


def prepare(a, mean, at):
    k, n = a.shape
    out = jax.ShapeDtypeStruct((k, n), jnp.bfloat16)
    spec = pl.BlockSpec((k // 8, n), lambda j, at: (j, 0))
    return pl.pallas_call(
        prepare_body,
        grid_spec=pltpu.PrefetchScalarGridSpec(
            num_scalar_prefetch=1,
            grid=(8,),
            in_specs=[spec, pl.BlockSpec((1, n), lambda j, at: (0, 0))],
            out_specs=[spec, spec],
        ),
        out_shape=[out, out],
        compiler_params=pltpu.CompilerParams(vmem_limit_bytes=VMEM),
        name="prepare",
    )(at, a, mean)


def gram_body(at_ref, mean_ref, *refs, terms, extra):
    k = pl.program_id(0)
    ins, refs = refs[: 3 * terms], refs[3 * terms :]
    if extra:
        sums, refs = refs[:4], refs[4:]
    norms, outs = refs[:terms], refs[terms:]
    dims = (((0,), (0,)), ((), ()))
    dot = lambda l, r: lax.dot_general(l, r, dims, preferred_element_type=jnp.float32)
    total = None
    for t in range(terms):
        a_ref, high_ref, low_ref = ins[3 * t : 3 * t + 3]
        a = a_ref[...] - mean_ref[...]
        norm = jnp.sum(a * a, axis=1, keepdims=True)

        @pl.when(k == 0)
        def _():
            norms[t][...] = norm

        @pl.when(k > 0)
        def _():
            norms[t][...] += norm

        high, low = high_low(a)
        part = dot(high, high_ref[...]) + (dot(high, low_ref[...]) + dot(low, high_ref[...]))
        total = part if total is None else total + part
    g = total.shape[0] // 2
    tile = lambda r, v, q: total[r * g : (r + 1) * g, (2 * v + q) * g : (2 * v + q + 1) * g]
    if extra:
        a_keep, a_away, b_keep, b_away = outs
        for v in range(4):
            ref = b_keep if v < 2 else b_away
            for q in range(2):
                ref[v % 2, 0, q] = tile(1, v, q)
            ref[v % 2, 0, 2] = sums[2][v, 0] + sums[3][v, 0]

        def put(ref):
            for v in range(4):
                for q in range(2):
                    ref[0, v, q] = tile(0, v, q)
                ref[0, v, 2] = sums[0][0, v] + sums[1][0, v]

        @pl.when(k < 2)
        def _():
            put(a_keep)

        @pl.when(k >= 2)
        def _():
            put(a_away)
    else:
        a_all, b_all, a_over, b_over = outs
        for v in range(4):
            w = (0, 2, 1, 3)[v]
            a_all[0, v] = tile(0, v, 0)
            b_all[v, 0] = tile(1, v, 1)
            a_over[0, w] = tile(0, v, 1)
            b_over[w, 0] = tile(1, v, 0)


def gram(lefts, mean, right, at, sums):
    terms = len(lefts)
    high, low = right
    n = high.shape[1]
    h = high.shape[0] // 2
    g = n // 8
    specs = [pl.BlockSpec((1, 2 * g), lambda k, at: (0, at[k]))]
    args = [mean]
    for t, left in enumerate(lefts):
        specs.append(pl.BlockSpec((h, 2 * g), lambda k, at, t=t: (at[4 + 2 * t], at[k])))
        row = pl.BlockSpec(
            (h, n), lambda k, at, t=t: (at[5 + 2 * t], 0), pipeline_mode=pl.Buffered(1)
        )
        specs += [row, row]
        args += [left, high, low]
    in_row = pl.BlockSpec((1, 4, g, g), lambda k, at: (k, 0, 0, 0))
    in_col = pl.BlockSpec((4, 1, g, g), lambda k, at: (0, k, 0, 0))
    shapes = [(h, 1)] * terms
    outs = [pl.BlockSpec((h, 1), lambda k, at: (0, 0))] * terms
    if sums:
        specs += [in_row, in_row, in_col, in_col]
        args += sums
        shapes += [(2, 4, 3, g, g)] * 4
        outs += [
            pl.BlockSpec((1, 4, 3, g, g), lambda k, at: (jnp.minimum(k, 1), 0, 0, 0, 0)),
            pl.BlockSpec((1, 4, 3, g, g), lambda k, at: (jnp.maximum(k - 2, 0), 0, 0, 0, 0)),
        ] + [pl.BlockSpec((2, 1, 3, g, g), lambda k, at: (0, k, 0, 0, 0))] * 2
    else:
        shapes += [(4, 4, g, g)] * 4
        outs += [
            in_row,
            in_col,
            pl.BlockSpec((1, 4, g, g), lambda k, at: (swapped(k), 0, 0, 0)),
            pl.BlockSpec((4, 1, g, g), lambda k, at: (0, swapped(k), 0, 0)),
        ]
    res = pl.pallas_call(
        functools.partial(gram_body, terms=terms, extra=bool(sums)),
        grid_spec=pltpu.PrefetchScalarGridSpec(
            num_scalar_prefetch=1, grid=(4,), in_specs=specs, out_specs=outs
        ),
        out_shape=[jax.ShapeDtypeStruct(i, jnp.float32) for i in shapes],
        cost_estimate=pl.CostEstimate(
            flops=6 * terms * h * n * n, bytes_accessed=8 * n * n, transcendentals=0
        ),
        compiler_params=pltpu.CompilerParams(vmem_limit_bytes=VMEM),
    )(at, *args)
    return res[:terms], res[terms:]


def flip_body(a_ref, out_ref):
    for i in range(a_ref.shape[0]):
        out_ref[i] = a_ref[i].T


def flip(a):
    return pl.pallas_call(
        flip_body,
        out_shape=jax.ShapeDtypeStruct(a.shape, jnp.float32),
        compiler_params=pltpu.CompilerParams(vmem_limit_bytes=VMEM),
        name="flip",
    )(a)


def combine_body(
    at_ref, pa, pb, qa, qb, d_got, p_got, q_got, p_own, p_other, q_left, q_right,
    norm0, norm1, near0, near1, far0, own_ref, out1, out2, out3, sums_ref, blocks,
    *, scenarios,
):
    c, e, h = at_ref[0], at_ref[1], at_ref[2]
    first = c == 0
    mine = lambda a, b: jnp.where(first, a, b)
    g = qa.shape[0]
    own = [mine(pa[i], pb[1 - i]) + p_own[i] for i in range(2)]
    other = [mine(p_got[1 - i], p_got[i]) + p_other[i] for i in range(2)]
    left = [
        mine(pa[2], pb[2]),
        mine(own[0], other[0]),
        mine(qa[...], qb[...]) + q_left[...],
        mine(other[0], own[0]),
    ]
    right = [
        d_got[...],
        mine(own[1], other[1]),
        q_got[...] + q_right[...],
        mine(other[1], own[1]),
    ]
    squares = None
    for i in range(4):
        for j, a in enumerate((left[i], right[i])):
            a = a * (1.0 / scenarios)
            blocks[i, :, j * g : (j + 1) * g] = a
            squares = a * a if squares is None else squares + a * a
    all_of = lambda a: jnp.sum(jnp.sum(a, axis=1, keepdims=True), axis=0, keepdims=True)
    frob = all_of(squares)
    n0, n1, m0, m1 = norm0[...], norm1[...], near0[...], near1[...]
    straight = n0 * m0 + n1 * m1
    crossed = n0 * m1 + n1 * m0
    far = jnp.where(h == 0, n0, n1) * far0[...]
    beta = all_of(n0 * n0 + n1 * n1 + 2.0 * (jnp.where(e == 0, straight, crossed) + far))
    trace = all_of(n0 + n1)
    lane = lax.broadcasted_iota(jnp.int32, (1, 128), 1)
    row = jnp.where(lane == 0, trace, jnp.where(lane == 1, beta, jnp.where(lane == 2, frob, 0.0)))
    sums_ref[...] = jnp.broadcast_to(row.reshape(1, 1, 128), sums_ref.shape)
    for i, ref in enumerate((own_ref, out1, out2, out3)):
        ref[...] = blocks[at_ref[3 + i]]


def combine(at, arrays, scenarios):
    g = arrays[2].shape[0]
    tile = jax.ShapeDtypeStruct((g, 2 * g), jnp.float32)
    return pl.pallas_call(
        functools.partial(combine_body, scenarios=scenarios),
        in_specs=[pl.BlockSpec(memory_space=pltpu.SMEM)]
        + [pl.BlockSpec(memory_space=pltpu.VMEM)] * len(arrays),
        out_shape=[tile] * 4 + [jax.ShapeDtypeStruct((128, 1, 128), jnp.float32)],
        scratch_shapes=[pltpu.VMEM((4, g, 2 * g), jnp.float32)],
        compiler_params=pltpu.CompilerParams(vmem_limit_bytes=VMEM),
        name="combine",
    )(at, *arrays)


def shrink_body(at_ref, own, got1, got2, got3, sums_ref, out_ref, *, scenarios, order):
    sums = jnp.sum(sums_ref[...], axis=0)
    lane = lax.broadcasted_iota(jnp.int32, sums.shape, 1)
    one = lambda i: jnp.sum(jnp.where(lane == i, sums, 0.0), axis=1, keepdims=True)
    trace_sum, beta_raw, frob_sum = one(0), one(1), one(2)
    target = trace_sum / (scenarios * order)
    beta_term = (beta_raw / scenarios - frob_sum) / (order * scenarios)
    delta_term = (frob_sum - order * target * target) / order
    shrinkage = beta_term / (delta_term + EPS)
    keep, add = 1.0 - shrinkage, shrinkage * target
    g, w = own.shape
    rows = lax.broadcasted_iota(jnp.int32, (g, w), 0)
    cols = lax.broadcasted_iota(jnp.int32, (g, w), 1)
    for i, ref in enumerate((own, got1, got2, got3)):
        at = at_ref[i]
        on = rows + at_ref[4] == cols + at * w
        to = pl.ds(pl.multiple_of(at * w, w), w)
        out_ref[:, to] = keep * ref[...] + jnp.where(on, add, 0.0)


def shrink(at, arrays, scenarios, order):
    g, w = arrays[0].shape
    return pl.pallas_call(
        functools.partial(shrink_body, scenarios=scenarios, order=order),
        in_specs=[pl.BlockSpec(memory_space=pltpu.SMEM)]
        + [pl.BlockSpec(memory_space=pltpu.VMEM)] * len(arrays),
        out_shape=jax.ShapeDtypeStruct((g, 4 * w), jnp.float32),
        compiler_params=pltpu.CompilerParams(vmem_limit_bytes=VMEM),
        name="shrink",
    )(at, *arrays)


def halve(keep, away, routes_of):
    total = keep + send(away, routes_of[0])
    return total[0] + send(total[1], routes_of[1])


def finish(parts):
    a = halve(parts[0], parts[1], Y_HALF)
    b = halve(parts[2], parts[3], X_HALF)
    a = halve(a[:2], a[2:], X_HALF)
    return a, halve(b[:2], b[2:], Y_HALF)


def from_core(parts):
    return [send(parts[2 + i], OTHER_CORE) for i in range(2)]


def on_device(returns):
    local, n = returns.shape
    g = n // 8
    half = local // 2
    scenarios = local * 32
    order = n * 4
    x, y, c, z = (lax.axis_index(a) for a in AXES)
    first = c == 0
    low_z = (z < 2).astype(jnp.int32)
    early_raw = send(lax.dynamic_slice_in_dim(returns, low_z * half, half), TO_Z)
    late_raw = send(lax.dynamic_slice_in_dim(returns, (1 - low_z) * half, half), TO_Z)
    far_raw = send(early_raw, TO_Z)
    sums = to_everyone(jnp.sum(returns, axis=0, keepdims=True), SCEN)
    mean = jnp.sum(sums, axis=0).reshape(1, n) / scenarios
    mean_near = send(mean, TO_Z)
    mean_far = send(mean, ACROSS)

    turn = [jnp.where(first, i, j) for i, j in ((0, 0), (3, 1), (1, 3), (2, 2))]
    ys = [y ^ i for i in turn]
    cols = [2 * (x ^ i) + k for i in turn for k in (c, 1 - c)]
    right = prepare(returns, mean, jnp.stack(cols))
    near_z = (z + jnp.where(first, 1, 3)) % 4
    near_early = (near_z < 2).astype(jnp.int32)
    far_half = 1 - low_z
    (norm0, norm1), d_parts = gram(
        [returns, returns], mean, right, jnp.stack(ys + [0, 0, 1, 1]), None
    )
    d_over = from_core(d_parts)
    (near0, near1), p_parts = gram(
        [early_raw, late_raw],
        mean_near,
        right,
        jnp.stack(ys + [0, near_early, 0, 1 - near_early]),
        [d_parts[0], d_over[0], d_parts[1], d_over[1]],
    )
    pa, pb = finish(p_parts)
    (far0,), q_parts = gram([far_raw], mean_far, right, jnp.stack(ys + [0, far_half]), None)
    q_over = from_core(q_parts)
    q_keep = [q_parts[i][:2] + q_over[i][:2] for i in range(2)]
    q_away = [q_parts[i][2:] + q_over[i][2:] for i in range(2)]
    q = finish([q_keep[0], q_away[0], q_keep[1], q_away[1]])

    mine = lambda a, b: jnp.where(first, a, b)
    d_got = send(mine(pb[2], pa[2]), OTHER_CORE)
    p_got = send(mine(pb[:2], pa[:2]), OTHER_CORE)
    p_flip = flip(jnp.stack([pa[0], pb[0], pa[1], pb[1]]))
    p_other = send(p_flip[:2], FLIP_NEAR[0])
    p_own = send(p_flip[2:], FLIP_NEAR[1])
    q_got = send(mine(q[1], q[0]), OTHER_CORE)
    q_flip = flip(jnp.stack(q))
    q_left = send(q_flip[0], FLIP_FAR[0])
    q_right = send(q_flip[1], FLIP_FAR[1])
    at = jnp.stack([c, near_early, far_half] + [((x ^ i) - z) % 4 for i in range(4)])
    *tiles, sums = combine(
        at,
        [pa, pb, q[0], q[1], d_got, p_got, q_got, p_own, p_other, q_left, q_right]
        + [norm0, norm1, near0, near1, far0],
        scenarios,
    )
    tiles = [tiles[0]] + [send(tiles[i], X_BY[i]) for i in (1, 2, 3)]
    sums = lax.all_to_all(sums, AXES, split_axis=0, concat_axis=0, tiled=True)
    row = (x - z) * n + (2 * y + c) * g
    at = jnp.stack([x, x ^ 1, x ^ 2, x ^ 3, row])
    return shrink(at, tiles + [sums], scenarios, order)


def solution(mesh):
    torus = Mesh(mesh.devices.reshape(4, 4, 2, 4), AXES)
    spec = P(SCEN, "z")

    return jax.shard_map(on_device, mesh=torus, in_specs=(spec,), out_specs=spec, check_vma=False)
```

time: 407 us -> 215 us (0.53)
  waiting for transfers between devices: 247 us -> 76.4 us
  starting transfers between devices: 7.13 us -> 74.7 us
  matrix products: 59.2 us -> 0 us
  blocking collectives: 49.3 us -> 0 us
  Pallas kernels: 0 us -> 33.2 us
  local copies, waits for them, and re-layouts: 1.27 us -> 22.5 us
  other arithmetic: 25.3 us -> 6.19 us
  between operations: 17.3 us -> 0.5 us
    all_gather x1 -> x0, waiting for transfers between devices: 153 us -> none  [on_device(): wide_rows = lax.all_gather(centered, 'own', axis=1, tiled=True)]
    reduce_scatter x1 -> x0, waiting for transfers between devices: 86.8 us -> none  [on_device(): lax.psum_scatter(product_over_scenarios(wide_rows, centered), SCEN, scatt...]
    ppermute x0 -> x35, waiting for transfers between devices: none -> 59.9 us  [send(): return lax.ppermute(a, AXES, route)]
    dot_general x1 -> x0, matrix products: 59.2 us -> none  [product_over_scenarios(): lax.dot_general(left_part, right_part, (((0,), (0,)), ((), ())), precisio...]
    ppermute x0 -> x35, starting transfers between devices: none -> 58.6 us  [send(): return lax.ppermute(a, AXES, route)]
    psum x4 -> x0, blocking collectives: 34.2 us -> none  [by_axis(): return functools.reduce(lax.psum, axes, array)]
    pallas_call x0 -> x8, Pallas kernels: none -> 33.2 us  [the longest x3 27.8 us: gram(): pl.pallas_call(functools.partial(gram_body, terms=terms, extra=bool(sums)...]
    all_to_all x1 -> x0, blocking collectives: 15.1 us -> none  [sent_to_all(): return lax.all_to_all(copies, axis, split_axis=0, concat_axis=0, tiled=True)]
  transfers between devices with their start and end apart: 3 -> 37, of which waited for: 3 -> 15; matrix products, arithmetic and copies ran while one was open for 4% -> 4% of each run, Pallas kernels for 0% -> 9%
where the time goes in v1:
time: 215 us; the launch traced here: 213 us
  waiting for transfers between devices  76.4 us (36%)
  starting transfers between devices  74.7 us (35%)
  Pallas kernels  33.2 us (15%)
  local copies, waits for them, and re-layouts  22.5 us (10%)
  other arithmetic  6.19 us (3%)
    ppermute x35, waiting for transfers between devices, send(): return lax.ppermute(a, AXES, route)  59.9 us
    ppermute x35, starting transfers between devices, send(): return lax.ppermute(a, AXES, route)  58.6 us
    pallas_call x3, Pallas kernels, gram(): pl.pallas_call(functools.partial(gram_body, terms=terms, extra=bool(sums)...  27.8 us
    unnamed x28, local copies, waits for them, and re-layouts  14.3 us
    all_to_all x1, waiting for transfers between devices, on_device(): sums = lax.all_to_all(sums, AXES, split_axis=0, concat_axis=0, tiled=True)  8.91 us
    all_to_all x1, starting transfers between devices, on_device(): sums = lax.all_to_all(sums, AXES, split_axis=0, concat_axis=0, tiled=True)  8.76 us
    all_to_all x1, waiting for transfers between devices, to_everyone(): return lax.all_to_all(copies, axes, split_axis=0, concat_axis=0, tiled=True)  7.6 us
    all_to_all x1, starting transfers between devices, to_everyone(): return lax.all_to_all(copies, axes, split_axis=0, concat_axis=0, tiled=True)  7.32 us
  transfers between devices with their start and end apart: 37, of which 15 were waited for; matrix products, arithmetic and copies ran while one was open for 4% of the time, Pallas kernels for 9%

profile of v1, /device:TPU:0, one launch (start us, length us, event | category | flops | bytes accessed | tf_op | source)
XLA Modules:
  0.0 213.4 jit_solution(7964198952400842795)
XLA Ops:
  0.0 4.9 %constant_dynamic-slice_fusion = (f32[512,1024]{1,0:T(8,128)}, f32[512,1024]{1,0:T(8,128)}) fusion(f32[1024,1024]{1,0:T(8,128)} %refs_3_.1, s32[]{:T(128)S(6)} %select_n.69, s32[]{:T(128)S(6)} %mul.34), kind=kLoop, calls=%fused_computation.43 | loop fusion | bytes 8388616 | tf_op jit(solution)/shard_map/dynamic_slice | solution.py:326
  4.9 4.1 %collective-permute-start.1 = (f32[512,1024]{1,0:T(8,128)}, f32[512,1024]{1,0:T(8,128)}, u32[]{:S(2)}, u32[]{:S(2)}) collective-permute-start(f32[512,1024]{1,0:T(8,128)} %get-tuple-element.57), channel_id=1, source_target_pairs={{0,3},{1,0},{2,1},{3,2},{4,5},{5,6},{6,7},{7,4},{8,11},{9,8},{10,9... | collective-permute-start | bytes 6291464 | tf_op jit(solution)/shard_map/ppermute | solution.py:46
  9.4 2.5 %reduce_sum.18 = f32[1024]{0:T(1024)S(1)} reduce(f32[1024,1024]{1,0:T(8,128)} %refs_3_.1, f32[]{:T(128)} %constant.65.clone.1), dimensions={0}, to_apply=%region_0.0 | reduce | flops 1047552 | bytes 4198404 | tf_op jit(solution)/shard_map/reduce_sum | solution.py:328
  12.6 7.3 %all-to-all-start = ((f32[32,1,1024]{2,1,0:T(1,128)}), f32[32,1,1024]{2,1,0:T(1,128)S(1)}, u32[]{:S(2)}, u32[]{:S(2)}) async-start(f32[32,1,1024]{2,1,0:T(1,128)} %broadcast_in_dim.4), calls=%async_computation | async-start | bytes 262144 | tf_op jit(solution)/shard_map/all_to_all | solution.py:51
  20.2 7.6 %all-to-all-done = f32[32,1,1024]{2,1,0:T(1,128)S(1)} async-done(((f32[32,1,1024]{2,1,0:T(1,128)}), f32[32,1,1024]{2,1,0:T(1,128)S(1)}, u32[]{:S(2)}, u32[]{:S(2)}) %all-to-all-start) | async-done | bytes 131104 | tf_op jit(solution)/shard_map/all_to_all | solution.py:51
  27.9 2.2 %copy-done = f32[1024,1024]{1,0:T(8,128)S(1)} copy-done((f32[1024,1024]{1,0:T(8,128)S(1)}, f32[1024,1024]{1,0:T(8,128)}, u32[]{:S(2)}) %copy-start) | copy-done | bytes 4194328
  30.1 1.7 prepare.1
  31.8 10.3 %shard_map.17 = (f32[512,1]{1,0:T(8,128)S(1)}, f32[512,1]{1,0:T(8,128)S(1)}, f32[4,4,128,128]{3,2,1,0:T(8,128)S(1)}, f32[4,4,128,128]{3,2,1,0:T(8,128)S(1)}, f32...) custom-call(s32[8]{0:T(128)S(1)} %stack.144.at_ref, f32[1,1024]{1,0:T(1,128)S(1)} %bitcast.87, ...), custom_call_target="tpu_custom_call" | custom-call | flops 6442450944 | bytes 8388608 | tf_op jit(solution)/shard_map/pallas_call | solution.py:182
  44.8 10.6 %collective-permute-done.mean_ref = f32[1,1024]{1,0:T(1,128)S(1)} collective-permute-done((f32[1,1024]{1,0:T(1,128)S(1)}, f32[1,1024]{1,0:T(1,128)S(1)}, u32[]{:S(2)}, u32[]{:S(2)}) %collective-permute-start) | collective-permute-done | bytes 4128 | tf_op jit(solution)/shard_map/ppermute | solution.py:46
  55.4 1.4 copy-done.1
  56.7 1.6 copy-done.2
  58.3 1.6 copy-done.4
  59.9 1.6 copy-done.7
  64.0 10.9 %shard_map.18 = (f32[512,1]{1,0:T(8,128)S(1)}, f32[512,1]{1,0:T(8,128)S(1)}, f32[2,4,3,128,128]{4,3,2,1,0:T(8,128)S(1)}, f32[2,4,3,128,128]{4,3,2,1,0:T(8,128)S(...) custom-call(s32[8]{0:T(128)S(1)} %stack.134.at_ref, ...), custom_call_target="tpu_custom_call" | custom-call | flops 6442450944 | bytes 8388608 | tf_op jit(solution)/shard_map/pallas_call | solution.py:182
  74.9 1.7 collective-permute-start.5
  76.6 1.5 collective-permute-start.9
  78.0 3.6 %collective-permute-start.14 = (f32[512,1024]{1,0:T(8,128)}, f32[512,1024]{1,0:T(8,128)}, u32[]{:S(2)}, u32[]{:S(2)}) collective-permute-start(f32[512,1024]{1,0:T(8,128)} %collective-permute-done.1.refs_0_), channel_id=1, source_target_pairs={{0,3},{1,0},{2,1},{3,2},{4,5},{5,6},{6,7},{7,4},{8,11},{9,8},{10,9... | collective-permute-start | bytes 6291464 | tf_op jit(solution)/shard_map/ppermute | solution.py:46
  81.7 13.7 %collective-permute-done.5 = f32[2,4,3,128,128]{4,3,2,1,0:T(8,128)S(1)} collective-permute-done((f32[2,4,3,128,128]{4,3,2,1,0:T(8,128)S(1)}, f32[2,4,3,128,128]{4,3,2,1,0:T(8,128)S(1)}, u32[]{:S(2)}, u32[]{:S(2)}) %collective-permute-start.5) | collective-permute-done | bytes 1572896 | tf_op jit(solution)/shard_map/ppermute | solution.py:46
  96.6 3.1 %collective-permute-start.6 = (f32[4,3,128,128]{3,2,1,0:T(8,128)}, f32[4,3,128,128]{3,2,1,0:T(8,128)}, u32[]{:S(2)}, u32[]{:S(2)}) collective-permute-start(f32[4,3,128,128]{3,2,1,0:T(8,128)} %slice_bitcast_fusion.2), channel_id=1, source_target_pairs={{0,24},{1,25},{2,26},{3,27},{4,12},{5,13},{6,14},{7,15},{8,16},{9,... | collective-permute-start | bytes 2359304 | tf_op jit(solution)/shard_map/ppermute | solution.py:46
  100.8 2.8 %collective-permute-start.10 = (f32[4,3,128,128]{3,2,1,0:T(8,128)}, f32[4,3,128,128]{3,2,1,0:T(8,128)}, u32[]{:S(2)}, u32[]{:S(2)}) collective-permute-start(f32[4,3,128,128]{3,2,1,0:T(8,128)} %slice_bitcast_fusion), channel_id=1, source_target_pairs={{0,96},{1,97},{2,98},{3,99},{4,36},{5,37},{6,38},{7,39},{8,104},{9... | collective-permute-start | bytes 2359304 | tf_op jit(solution)/shard_map/ppermute | solution.py:46
  103.6 2.3 %collective-permute-start.13 = (f32[1,1024]{1,0:T(1,128)S(1)}, f32[1,1024]{1,0:T(1,128)S(1)}, u32[]{:S(2)}, u32[]{:S(2)}) collective-permute-start(f32[1,1024]{1,0:T(1,128)S(1)} %bitcast.89), channel_id=1, source_target_pairs={{0,2},{1,3},{2,0},{3,1},{4,6},{5,7},{6,4},{7,5},{8,10},{9,11},{10,... | collective-permute-start | bytes 12296 | tf_op jit(solution)/shard_map/ppermute | solution.py:46
  105.9 4.2 %collective-permute-done.6 = f32[4,3,128,128]{3,2,1,0:T(8,128)} collective-permute-done((f32[4,3,128,128]{3,2,1,0:T(8,128)}, f32[4,3,128,128]{3,2,1,0:T(8,128)}, u32[]{:S(2)}, u32[]{:S(2)}) %collective-permute-start.6) | collective-permute-done | bytes 786464 | tf_op jit(solution)/shard_map/ppermute | solution.py:46
  110.1 1.5 fusion.1
  111.6 1.6 collective-permute-start.7
  113.2 1.6 copy-done.8
  114.8 6.6 %shard_map.19 = (f32[512,1]{1,0:T(8,128)S(1)}, f32[4,4,128,128]{3,2,1,0:T(8,128)S(1)}, f32[4,4,128,128]{3,2,1,0:T(8,128)S(1)}, f32[4,4,128,128]{3,2,1,0:T(8,128)S(1)}, f32[4,4,128,128]{3,2,1,0:T(8,128)S(1)}) custom-call(s32[6]{0:T(128)S(1)} %stack.145.at_ref, f32[1,1024]{1,0:T(1,128)S(1)} %collective-permute-done.13.mean_ref, ...), custom_call_target="tpu_custom_call" | custom-call | flops 3221225472 | bytes 8388608 | tf_op jit(solution)/shard_map/pallas_call | solution.py:182
  123.8 2.2 %collective-permute-start.8 = (f32[3,128,128]{2,1,0:T(8,128)S(1)}, f32[3,128,128]{2,1,0:T(8,128)S(1)}, u32[]{:S(2)}, u32[]{:S(2)}) collective-permute-start(f32[3,128,128]{2,1,0:T(8,128)S(1)} %slice_bitcast_fusion.10), channel_id=1, source_target_pairs={{0,96},{1,97},{2,98},{3,99},{4,36},{5,37},{6,38},{7,39},{8,104},{9... | collective-permute-start | bytes 589832 | tf_op jit(solution)/shard_map/ppermute | solution.py:46
  126.0 5.1 %collective-permute-done.11 = f32[2,3,128,128]{3,2,1,0:T(8,128)S(1)} collective-permute-done((f32[2,3,128,128]{3,2,1,0:T(8,128)S(1)}, f32[2,3,128,128]{3,2,1,0:T(8,128)S(1)}, u32[]{:S(2)}, u32[]{:S(2)}) %collective-permute-start.11) | collective-permute-done | bytes 393248 | tf_op jit(solution)/shard_map/ppermute | solution.py:46
  131.2 3.3 %collective-permute-start.12 = (f32[3,128,128]{2,1,0:T(8,128)S(1)}, f32[3,128,128]{2,1,0:T(8,128)S(1)}, u32[]{:S(2)}, u32[]{:S(2)}) collective-permute-start(f32[3,128,128]{2,1,0:T(8,128)S(1)} %slice_bitcast_fusion.8), channel_id=1, source_target_pairs={{0,24},{1,25},{2,26},{3,27},{4,12},{5,13},{6,14},{7,15},{8,16},{9,... | collective-permute-start | bytes 589832 | tf_op jit(solution)/shard_map/ppermute | solution.py:46
  134.5 3.8 %collective-permute-done.12 = f32[3,128,128]{2,1,0:T(8,128)S(1)} collective-permute-done((f32[3,128,128]{2,1,0:T(8,128)S(1)}, f32[3,128,128]{2,1,0:T(8,128)S(1)}, u32[]{:S(2)}, u32[]{:S(2)}) %collective-permute-start.12) | collective-permute-done | bytes 196640 | tf_op jit(solution)/shard_map/ppermute | solution.py:46
  139.2 2.2 %collective-permute-start.25 = (f32[128,128]{1,0:T(8,128)S(1)}, f32[128,128]{1,0:T(8,128)S(1)}, u32[]{:S(2)}, u32[]{:S(2)}) collective-permute-start(f32[128,128]{1,0:T(8,128)S(1)} %get-tuple-element.62), channel_id=1, source_target_pairs={{0,4},{1,5},{2,6},{3,7},{4,0},{5,1},{6,2},{7,3},{8,12},{9,13},{10,... | collective-permute-start | bytes 196616 | tf_op jit(solution)/shard_map/ppermute | solution.py:46
  141.5 6.2 %collective-permute-done.21 = f32[2,4,128,128]{3,2,1,0:T(8,128)S(1)} collective-permute-done((f32[2,4,128,128]{3,2,1,0:T(8,128)S(1)}, f32[2,4,128,128]{3,2,1,0:T(8,128)S(1)}, u32[]{:S(2)}, u32[]{:S(2)}) %collective-permute-start.21) | collective-permute-done | bytes 524320 | tf_op jit(solution)/shard_map/ppermute | solution.py:46
  147.8 2.2 %collective-permute-start.22 = (f32[4,128,128]{2,1,0:T(8,128)S(1)}, f32[4,128,128]{2,1,0:T(8,128)S(1)}, u32[]{:S(2)}, u32[]{:S(2)}) collective-permute-start(f32[4,128,128]{2,1,0:T(8,128)S(1)} %slice_bitcast_fusion.4), channel_id=1, source_target_pairs={{0,96},{1,97},{2,98},{3,99},{4,36},{5,37},{6,38},{7,39},{8,104},{9... | collective-permute-start | bytes 786440 | tf_op jit(solution)/shard_map/ppermute | solution.py:46
  150.1 3.1 %collective-permute-start.17 = (f32[4,128,128]{2,1,0:T(8,128)S(1)}, f32[4,128,128]{2,1,0:T(8,128)S(1)}, u32[]{:S(2)}, u32[]{:S(2)}) collective-permute-start(f32[4,128,128]{2,1,0:T(8,128)S(1)} %slice_bitcast_fusion.6), channel_id=1, source_target_pairs={{0,24},{1,25},{2,26},{3,27},{4,12},{5,13},{6,14},{7,15},{8,16},{9,... | collective-permute-start | bytes 786440 | tf_op jit(solution)/shard_map/ppermute | solution.py:46
  153.3 2.1 collective-permute-done.22
  155.6 3.5 %collective-permute-done.17 = f32[4,128,128]{2,1,0:T(8,128)S(1)} collective-permute-done((f32[4,128,128]{2,1,0:T(8,128)S(1)}, f32[4,128,128]{2,1,0:T(8,128)S(1)}, u32[]{:S(2)}, u32[]{:S(2)}) %collective-permute-start.17) | collective-permute-done | bytes 262176 | tf_op jit(solution)/shard_map/ppermute | solution.py:46
  160.6 3.1 %collective-permute-start.24 = (f32[128,128]{1,0:T(8,128)S(1)}, f32[128,128]{1,0:T(8,128)S(1)}, u32[]{:S(2)}, u32[]{:S(2)}) collective-permute-start(f32[128,128]{1,0:T(8,128)S(1)} %slice_bitcast_fusion.14), channel_id=1, source_target_pairs={{0,24},{1,25},{2,26},{3,27},{4,12},{5,13},{6,14},{7,15},{8,16},{9,... | collective-permute-start | bytes 196616 | tf_op jit(solution)/shard_map/ppermute | solution.py:46
  164.3 2.0 collective-permute-start.19
  166.7 4.0 %collective-permute-done.19 = f32[128,128]{1,0:T(8,128)S(1)} collective-permute-done((f32[128,128]{1,0:T(8,128)S(1)}, f32[128,128]{1,0:T(8,128)S(1)}, u32[]{:S(2)}, u32[]{:S(2)}) %collective-permute-start.19) | collective-permute-done | bytes 65568 | tf_op jit(solution)/shard_map/ppermute | solution.py:46
  171.0 4.2 %collective-permute-start.30 = (f32[128,128]{1,0:T(8,128)S(1)}, f32[128,128]{1,0:T(8,128)S(1)}, u32[]{:S(2)}, u32[]{:S(2)}) collective-permute-start(f32[128,128]{1,0:T(8,128)S(1)} %get-tuple-element.66), channel_id=1, source_target_pairs={{0,2},{1,3},{2,0},{3,1},{4,6},{5,7},{6,4},{7,5},{8,34},{9,35},{10,... | collective-permute-start | bytes 196616 | tf_op jit(solution)/shard_map/ppermute | solution.py:46
  175.5 2.4 %collective-permute-done.30.q_left = f32[128,128]{1,0:T(8,128)S(1)} collective-permute-done((f32[128,128]{1,0:T(8,128)S(1)}, f32[128,128]{1,0:T(8,128)S(1)}, u32[]{:S(2)}, u32[]{:S(2)}) %collective-permute-start.30) | collective-permute-done | bytes 65568 | tf_op jit(solution)/shard_map/ppermute | solution.py:46
  178.0 2.8 %collective-permute-done.31.q_right = f32[128,128]{1,0:T(8,128)S(1)} collective-permute-done((f32[128,128]{1,0:T(8,128)S(1)}, f32[128,128]{1,0:T(8,128)S(1)}, u32[]{:S(2)}, u32[]{:S(2)}) %collective-permute-start.31) | collective-permute-done | bytes 65568 | tf_op jit(solution)/shard_map/ppermute | solution.py:46
  180.7 1.8 combine.1
  182.5 3.6 %collective-permute-start.32 = (f32[128,256]{1,0:T(8,128)S(1)}, f32[128,256]{1,0:T(8,128)S(1)}, u32[]{:S(2)}, u32[]{:S(2)}) collective-permute-start(f32[128,256]{1,0:T(8,128)S(1)} %get-tuple-element.49), channel_id=1, source_target_pairs={{0,32},{1,33},{2,34},{3,35},{4,36},{5,37},{6,38},{7,39},{8,40},{9,... | collective-permute-start | bytes 393224 | tf_op jit(solution)/shard_map/ppermute | solution.py:46
  186.1 7.9 %collective-permute-start.33 = (f32[128,256]{1,0:T(8,128)S(1)}, f32[128,256]{1,0:T(8,128)S(1)}, u32[]{:S(2)}, u32[]{:S(2)}) collective-permute-start(f32[128,256]{1,0:T(8,128)S(1)} %get-tuple-element.50), channel_id=1, source_target_pairs={{0,64},{1,65},{2,66},{3,67},{4,68},{5,69},{6,70},{7,71},{8,72},{9,... | collective-permute-start | bytes 393224 | tf_op jit(solution)/shard_map/ppermute | solution.py:46
  194.0 8.8 %all-to-all-start.1 = ((f32[128,1,128]{2,1,0:T(1,128)}), f32[128,1,128]{2,1,0:T(1,128)S(1)}, u32[]{:S(2)}, u32[]{:S(2)}) async-start(f32[128,1,128]{2,1,0:T(1,128)} %get-tuple-element.52), calls=%async_computation.1 | async-start | bytes 131072 | tf_op jit(solution)/shard_map/all_to_all | solution.py:376
  202.9 8.9 %all-to-all-done.1.sums_ref = f32[128,1,128]{2,1,0:T(1,128)S(1)} async-done(((f32[128,1,128]{2,1,0:T(1,128)}), f32[128,1,128]{2,1,0:T(1,128)S(1)}, u32[]{:S(2)}, u32[]{:S(2)}) %all-to-all-start.1) | async-done | bytes 65568 | tf_op jit(solution)/shard_map/all_to_all | solution.py:376
  211.8 1.6 shrink.1
  (110 shorter events, 15.9 us)
Async XLA Ops:
  4.9 50.5 %collective-permute-start.1 = (f32[512,1024]{1,0:T(8,128)}, f32[512,1024]{1,0:T(8,128)}, u32[]{:S(2)}, u32[]{:S(2)}) collective-permute-start(f32[512,1024]{1,0:T(8,128)} %get-tuple-element.57), channel_id=1, source_target_pairs={{0,3},{1,0},{2,1},{3,2},{4,5},{5,6},{6,7},{7,4},{8,11},{9,8},{10,9... | collective-permute-start | bytes 6291464 | tf_op jit(solution)/shard_map/ppermute | solution.py:46
  9.0 46.4 %collective-permute-start.2 = (f32[512,1024]{1,0:T(8,128)}, f32[512,1024]{1,0:T(8,128)S(1)}, u32[]{:S(2)}, u32[]{:S(2)}) collective-permute-start(f32[512,1024]{1,0:T(8,128)} %get-tuple-element.56), channel_id=1, source_target_pairs={{0,3},{1,0},{2,1},{3,2},{4,5},{5,6},{6,7},{7,4},{8,11},{9,8},{10,9... | collective-permute-start | bytes 6291464 | tf_op jit(solution)/shard_map/ppermute | solution.py:46
  12.6 15.2 %all-to-all-start = ((f32[32,1,1024]{2,1,0:T(1,128)}), f32[32,1,1024]{2,1,0:T(1,128)S(1)}, u32[]{:S(2)}, u32[]{:S(2)}) async-start(f32[32,1,1024]{2,1,0:T(1,128)} %broadcast_in_dim.4), calls=%async_computation | async-start | bytes 262144 | tf_op jit(solution)/shard_map/all_to_all | solution.py:51
  27.9 2.2 %copy-start = (f32[1024,1024]{1,0:T(8,128)S(1)}, f32[1024,1024]{1,0:T(8,128)}, u32[]{:S(2)}) copy-start(f32[1024,1024]{1,0:T(8,128)} %refs_3_.1) | copy-start | bytes 12582916
  31.8 10.3 %copy-start.3 = (bf16[1024,1024]{1,0:T(8,128)(2,1)}, bf16[1024,1024]{1,0:T(8,128)(2,1)S(1)}, u32[]{:S(2)}) copy-start(bf16[1024,1024]{1,0:T(8,128)(2,1)S(1)} %get-tuple-element.29.refs_1_.refs_4_) | copy-start | bytes 6291460
  31.8 10.3 %copy-start.6 = (bf16[1024,1024]{1,0:T(8,128)(2,1)}, bf16[1024,1024]{1,0:T(8,128)(2,1)S(1)}, u32[]{:S(2)}) copy-start(bf16[1024,1024]{1,0:T(8,128)(2,1)S(1)} %get-tuple-element.30.refs_2_.refs_5_) | copy-start | bytes 6291460
  44.1 11.3 %collective-permute-start.3 = (f32[4,4,128,128]{3,2,1,0:T(8,128)}, f32[4,4,128,128]{3,2,1,0:T(8,128)}, u32[]{:S(2)}, u32[]{:S(2)}) collective-permute-start(f32[4,4,128,128]{3,2,1,0:T(8,128)} %get-tuple-element.32), channel_id=1, source_target_pairs={{0,4},{1,5},{2,6},{3,7},{4,0},{5,1},{6,2},{7,3},{8,12},{9,13},{10,... | collective-permute-start | bytes 3145736 | tf_op jit(solution)/shard_map/ppermute | solution.py:46
  44.2 11.2 %collective-permute-start.4 = (f32[4,4,128,128]{3,2,1,0:T(8,128)}, f32[4,4,128,128]{3,2,1,0:T(8,128)}, u32[]{:S(2)}, u32[]{:S(2)}) collective-permute-start(f32[4,4,128,128]{3,2,1,0:T(8,128)} %get-tuple-element.34), channel_id=1, source_target_pairs={{0,4},{1,5},{2,6},{3,7},{4,0},{5,1},{6,2},{7,3},{8,12},{9,13},{10,... | collective-permute-start | bytes 3145736 | tf_op jit(solution)/shard_map/ppermute | solution.py:46
  44.6 10.8 %collective-permute-start = (f32[1,1024]{1,0:T(1,128)S(1)}, f32[1,1024]{1,0:T(1,128)S(1)}, u32[]{:S(2)}, u32[]{:S(2)}) collective-permute-start(f32[1,1024]{1,0:T(1,128)S(1)} %bitcast.88), channel_id=1, source_target_pairs={{0,3},{1,0},{2,1},{3,2},{4,5},{5,6},{6,7},{7,4},{8,11},{9,8},{10,9... | collective-permute-start | bytes 12296 | tf_op jit(solution)/shard_map/ppermute | solution.py:46
  55.4 1.4 copy-start.1
  56.7 1.6 copy-start.2
  58.3 1.6 copy-start.4
  59.9 1.6 copy-start.7
  61.5 1.2 copy-start.10
  74.9 20.5 %collective-permute-start.5 = (f32[2,4,3,128,128]{4,3,2,1,0:T(8,128)S(1)}, f32[2,4,3,128,128]{4,3,2,1,0:T(8,128)S(1)}, u32[]{:S(2)}, u32[]{:S(2)}) collective-permute-start(f32[2,4,3,128,128]{4,3,2,1,0:T(8,128)S(1)} %get-tuple-element.36), channel_id=1, source_target_pairs={{0,8},{1,9},{2,10},{3,11},{4,28},{5,29},{6,30},{7,31},{8,0},{9,1},... | collective-permute-start | bytes 4718600 | tf_op jit(solution)/shard_map/ppermute | solution.py:46
  76.6 23.1 %collective-permute-start.9 = (f32[2,4,3,128,128]{4,3,2,1,0:T(8,128)S(1)}, f32[2,4,3,128,128]{4,3,2,1,0:T(8,128)S(1)}, u32[]{:S(2)}, u32[]{:S(2)}) collective-permute-start(f32[2,4,3,128,128]{4,3,2,1,0:T(8,128)S(1)} %get-tuple-element.38), channel_id=1, source_target_pairs={{0,32},{1,33},{2,34},{3,35},{4,100},{5,101},{6,102},{7,103},{8,40}... | collective-permute-start | bytes 4718600 | tf_op jit(solution)/shard_map/ppermute | solution.py:46
  78.0 35.1 %collective-permute-start.14 = (f32[512,1024]{1,0:T(8,128)}, f32[512,1024]{1,0:T(8,128)}, u32[]{:S(2)}, u32[]{:S(2)}) collective-permute-start(f32[512,1024]{1,0:T(8,128)} %collective-permute-done.1.refs_0_), channel_id=1, source_target_pairs={{0,3},{1,0},{2,1},{3,2},{4,5},{5,6},{6,7},{7,4},{8,11},{9,8},{10,9... | collective-permute-start | bytes 6291464 | tf_op jit(solution)/shard_map/ppermute | solution.py:46
  95.6 4.3 %copy-start.13 = (f32[2,4,3,128,128]{4,3,2,1,0:T(8,128)}, f32[2,4,3,128,128]{4,3,2,1,0:T(8,128)S(1)}, u32[]{:S(2)}) copy-start(f32[2,4,3,128,128]{4,3,2,1,0:T(8,128)S(1)} %add.130) | copy-start | bytes 4718596
  96.6 13.5 %collective-permute-start.6 = (f32[4,3,128,128]{3,2,1,0:T(8,128)}, f32[4,3,128,128]{3,2,1,0:T(8,128)}, u32[]{:S(2)}, u32[]{:S(2)}) collective-permute-start(f32[4,3,128,128]{3,2,1,0:T(8,128)} %slice_bitcast_fusion.2), channel_id=1, source_target_pairs={{0,24},{1,25},{2,26},{3,27},{4,12},{5,13},{6,14},{7,15},{8,16},{9,... | collective-permute-start | bytes 2359304 | tf_op jit(solution)/shard_map/ppermute | solution.py:46
  100.8 21.2 %collective-permute-start.10 = (f32[4,3,128,128]{3,2,1,0:T(8,128)}, f32[4,3,128,128]{3,2,1,0:T(8,128)}, u32[]{:S(2)}, u32[]{:S(2)}) collective-permute-start(f32[4,3,128,128]{3,2,1,0:T(8,128)} %slice_bitcast_fusion), channel_id=1, source_target_pairs={{0,96},{1,97},{2,98},{3,99},{4,36},{5,37},{6,38},{7,39},{8,104},{9... | collective-permute-start | bytes 2359304 | tf_op jit(solution)/shard_map/ppermute | solution.py:46
  103.6 9.6 %copy-start.5 = (bf16[1024,1024]{1,0:T(8,128)(2,1)S(1)}, bf16[1024,1024]{1,0:T(8,128)(2,1)}, u32[]{:S(2)}) copy-start(bf16[1024,1024]{1,0:T(8,128)(2,1)} %copy-done.3) | copy-start | bytes 6291460
  103.6 9.6 %collective-permute-start.13 = (f32[1,1024]{1,0:T(1,128)S(1)}, f32[1,1024]{1,0:T(1,128)S(1)}, u32[]{:S(2)}, u32[]{:S(2)}) collective-permute-start(f32[1,1024]{1,0:T(1,128)S(1)} %bitcast.89), channel_id=1, source_target_pairs={{0,2},{1,3},{2,0},{3,1},{4,6},{5,7},{6,4},{7,5},{8,10},{9,11},{10,... | collective-permute-start | bytes 12296 | tf_op jit(solution)/shard_map/ppermute | solution.py:46
  111.6 12.1 %collective-permute-start.7 = (f32[2,3,128,128]{3,2,1,0:T(8,128)S(1)}, f32[2,3,128,128]{3,2,1,0:T(8,128)S(1)}, u32[]{:S(2)}, u32[]{:S(2)}) collective-permute-start(f32[2,3,128,128]{3,2,1,0:T(8,128)S(1)} %slice.179), channel_id=1, source_target_pairs={{0,32},{1,33},{2,34},{3,35},{4,100},{5,101},{6,102},{7,103},{8,40}... | collective-permute-start | bytes 1179656 | tf_op jit(solution)/shard_map/ppermute | solution.py:46
  113.2 1.6 copy-start.8
  121.4 16.9 %collective-permute-start.20 = (f32[4,4,128,128]{3,2,1,0:T(8,128)S(1)}, f32[4,4,128,128]{3,2,1,0:T(8,128)S(1)}, u32[]{:S(2)}, u32[]{:S(2)}) collective-permute-start(f32[4,4,128,128]{3,2,1,0:T(8,128)S(1)} %get-tuple-element.42), channel_id=1, source_target_pairs={{0,4},{1,5},{2,6},{3,7},{4,0},{5,1},{6,2},{7,3},{8,12},{9,13},{10,... | collective-permute-start | bytes 3145736 | tf_op jit(solution)/shard_map/ppermute | solution.py:46
  121.5 17.6 %collective-permute-start.15 = (f32[4,4,128,128]{3,2,1,0:T(8,128)S(1)}, f32[4,4,128,128]{3,2,1,0:T(8,128)S(1)}, u32[]{:S(2)}, u32[]{:S(2)}) collective-permute-start(f32[4,4,128,128]{3,2,1,0:T(8,128)S(1)} %get-tuple-element.40), channel_id=1, source_target_pairs={{0,4},{1,5},{2,6},{3,7},{4,0},{5,1},{6,2},{7,3},{8,12},{9,13},{10,... | collective-permute-start | bytes 3145736 | tf_op jit(solution)/shard_map/ppermute | solution.py:46
  123.2 7.9 %collective-permute-start.11 = (f32[2,3,128,128]{3,2,1,0:T(8,128)S(1)}, f32[2,3,128,128]{3,2,1,0:T(8,128)S(1)}, u32[]{:S(2)}, u32[]{:S(2)}) collective-permute-start(f32[2,3,128,128]{3,2,1,0:T(8,128)S(1)} %slice.185), channel_id=1, source_target_pairs={{0,8},{1,9},{2,10},{3,11},{4,28},{5,29},{6,30},{7,31},{8,0},{9,1},... | collective-permute-start | bytes 1179656 | tf_op jit(solution)/shard_map/ppermute | solution.py:46
  123.8 10.7 %collective-permute-start.8 = (f32[3,128,128]{2,1,0:T(8,128)S(1)}, f32[3,128,128]{2,1,0:T(8,128)S(1)}, u32[]{:S(2)}, u32[]{:S(2)}) collective-permute-start(f32[3,128,128]{2,1,0:T(8,128)S(1)} %slice_bitcast_fusion.10), channel_id=1, source_target_pairs={{0,96},{1,97},{2,98},{3,99},{4,36},{5,37},{6,38},{7,39},{8,104},{9... | collective-permute-start | bytes 589832 | tf_op jit(solution)/shard_map/ppermute | solution.py:46
  131.2 7.1 %collective-permute-start.12 = (f32[3,128,128]{2,1,0:T(8,128)S(1)}, f32[3,128,128]{2,1,0:T(8,128)S(1)}, u32[]{:S(2)}, u32[]{:S(2)}) collective-permute-start(f32[3,128,128]{2,1,0:T(8,128)S(1)} %slice_bitcast_fusion.8), channel_id=1, source_target_pairs={{0,24},{1,25},{2,26},{3,27},{4,12},{5,13},{6,14},{7,15},{8,16},{9,... | collective-permute-start | bytes 589832 | tf_op jit(solution)/shard_map/ppermute | solution.py:46
  138.4 9.3 %collective-permute-start.21 = (f32[2,4,128,128]{3,2,1,0:T(8,128)S(1)}, f32[2,4,128,128]{3,2,1,0:T(8,128)S(1)}, u32[]{:S(2)}, u32[]{:S(2)}) collective-permute-start(f32[2,4,128,128]{3,2,1,0:T(8,128)S(1)} %slice_add_fusion), channel_id=1, source_target_pairs={{0,32},{1,33},{2,34},{3,35},{4,100},{5,101},{6,102},{7,103},{8,40}... | collective-permute-start | bytes 1572872 | tf_op jit(solution)/shard_map/ppermute | solution.py:46
  139.1 10.8 %collective-permute-start.16 = (f32[2,4,128,128]{3,2,1,0:T(8,128)S(1)}, f32[2,4,128,128]{3,2,1,0:T(8,128)S(1)}, u32[]{:S(2)}, u32[]{:S(2)}) collective-permute-start(f32[2,4,128,128]{3,2,1,0:T(8,128)S(1)} %slice_add_fusion.2), channel_id=1, source_target_pairs={{0,8},{1,9},{2,10},{3,11},{4,28},{5,29},{6,30},{7,31},{8,0},{9,1},... | collective-permute-start | bytes 1572872 | tf_op jit(solution)/shard_map/ppermute | solution.py:46
  139.2 31.8 %collective-permute-start.25 = (f32[128,128]{1,0:T(8,128)S(1)}, f32[128,128]{1,0:T(8,128)S(1)}, u32[]{:S(2)}, u32[]{:S(2)}) collective-permute-start(f32[128,128]{1,0:T(8,128)S(1)} %get-tuple-element.62), channel_id=1, source_target_pairs={{0,4},{1,5},{2,6},{3,7},{4,0},{5,1},{6,2},{7,3},{8,12},{9,13},{10,... | collective-permute-start | bytes 196616 | tf_op jit(solution)/shard_map/ppermute | solution.py:46
  141.4 33.8 %collective-permute-start.26 = (f32[2,128,128]{2,1,0:T(8,128)S(1)}, f32[2,128,128]{2,1,0:T(8,128)S(1)}, u32[]{:S(2)}, u32[]{:S(2)}) collective-permute-start(f32[2,128,128]{2,1,0:T(8,128)S(1)} %slice_select_fusion), channel_id=1, source_target_pairs={{0,4},{1,5},{2,6},{3,7},{4,0},{5,1},{6,2},{7,3},{8,12},{9,13},{10,... | collective-permute-start | bytes 393224 | tf_op jit(solution)/shard_map/ppermute | solution.py:46
  147.8 7.7 %collective-permute-start.22 = (f32[4,128,128]{2,1,0:T(8,128)S(1)}, f32[4,128,128]{2,1,0:T(8,128)S(1)}, u32[]{:S(2)}, u32[]{:S(2)}) collective-permute-start(f32[4,128,128]{2,1,0:T(8,128)S(1)} %slice_bitcast_fusion.4), channel_id=1, source_target_pairs={{0,96},{1,97},{2,98},{3,99},{4,36},{5,37},{6,38},{7,39},{8,104},{9... | collective-permute-start | bytes 786440 | tf_op jit(solution)/shard_map/ppermute | solution.py:46
  150.1 9.1 %collective-permute-start.17 = (f32[4,128,128]{2,1,0:T(8,128)S(1)}, f32[4,128,128]{2,1,0:T(8,128)S(1)}, u32[]{:S(2)}, u32[]{:S(2)}) collective-permute-start(f32[4,128,128]{2,1,0:T(8,128)S(1)} %slice_bitcast_fusion.6), channel_id=1, source_target_pairs={{0,24},{1,25},{2,26},{3,27},{4,12},{5,13},{6,14},{7,15},{8,16},{9,... | collective-permute-start | bytes 786440 | tf_op jit(solution)/shard_map/ppermute | solution.py:46
  155.5 5.0 %collective-permute-start.23 = (f32[2,128,128]{2,1,0:T(8,128)S(1)}, f32[2,128,128]{2,1,0:T(8,128)S(1)}, u32[]{:S(2)}, u32[]{:S(2)}) collective-permute-start(f32[2,128,128]{2,1,0:T(8,128)S(1)} %slice.201), channel_id=1, source_target_pairs={{0,8},{1,9},{2,10},{3,11},{4,28},{5,29},{6,30},{7,31},{8,0},{9,1},... | collective-permute-start | bytes 393224 | tf_op jit(solution)/shard_map/ppermute | solution.py:46
  159.2 5.0 %collective-permute-start.18 = (f32[2,128,128]{2,1,0:T(8,128)S(1)}, f32[2,128,128]{2,1,0:T(8,128)S(1)}, u32[]{:S(2)}, u32[]{:S(2)}) collective-permute-start(f32[2,128,128]{2,1,0:T(8,128)S(1)} %slice.193), channel_id=1, source_target_pairs={{0,32},{1,33},{2,34},{3,35},{4,100},{5,101},{6,102},{7,103},{8,40}... | collective-permute-start | bytes 393224 | tf_op jit(solution)/shard_map/ppermute | solution.py:46
  160.6 5.8 %collective-permute-start.24 = (f32[128,128]{1,0:T(8,128)S(1)}, f32[128,128]{1,0:T(8,128)S(1)}, u32[]{:S(2)}, u32[]{:S(2)}) collective-permute-start(f32[128,128]{1,0:T(8,128)S(1)} %slice_bitcast_fusion.14), channel_id=1, source_target_pairs={{0,24},{1,25},{2,26},{3,27},{4,12},{5,13},{6,14},{7,15},{8,16},{9,... | collective-permute-start | bytes 196616 | tf_op jit(solution)/shard_map/ppermute | solution.py:46
  164.3 6.5 %collective-permute-start.19 = (f32[128,128]{1,0:T(8,128)S(1)}, f32[128,128]{1,0:T(8,128)S(1)}, u32[]{:S(2)}, u32[]{:S(2)}) collective-permute-start(f32[128,128]{1,0:T(8,128)S(1)} %slice_bitcast_fusion.16), channel_id=1, source_target_pairs={{0,96},{1,97},{2,98},{3,99},{4,36},{5,37},{6,38},{7,39},{8,104},{9... | collective-permute-start | bytes 196616 | tf_op jit(solution)/shard_map/ppermute | solution.py:46
  166.3 9.2 %collective-permute-start.28 = (f32[2,128,128]{2,1,0:T(8,128)S(1)}, f32[2,128,128]{2,1,0:T(8,128)S(1)}, u32[]{:S(2)}, u32[]{:S(2)}) collective-permute-start(f32[2,128,128]{2,1,0:T(8,128)S(1)} %get-tuple-element.59), channel_id=1, source_target_pairs={{0,5},{1,6},{2,7},{3,4},{4,3},{5,0},{6,1},{7,2},{8,37},{9,38},{10,... | collective-permute-start | bytes 393224 | tf_op jit(solution)/shard_map/ppermute | solution.py:46
  166.4 9.1 %collective-permute-start.29 = (f32[2,128,128]{2,1,0:T(8,128)S(1)}, f32[2,128,128]{2,1,0:T(8,128)S(1)}, u32[]{:S(2)}, u32[]{:S(2)}) collective-permute-start(f32[2,128,128]{2,1,0:T(8,128)S(1)} %get-tuple-element.58), channel_id=1, source_target_pairs={{0,1},{1,2},{2,3},{3,0},{4,7},{5,4},{6,5},{7,6},{8,33},{9,34},{10,... | collective-permute-start | bytes 393224 | tf_op jit(solution)/shard_map/ppermute | solution.py:46
  170.8 4.7 %collective-permute-start.27 = (f32[128,128]{1,0:T(8,128)S(1)}, f32[128,128]{1,0:T(8,128)S(1)}, u32[]{:S(2)}, u32[]{:S(2)}) collective-permute-start(f32[128,128]{1,0:T(8,128)S(1)} %get-tuple-element.53), channel_id=1, source_target_pairs={{0,4},{1,5},{2,6},{3,7},{4,0},{5,1},{6,2},{7,3},{8,12},{9,13},{10,... | collective-permute-start | bytes 196616 | tf_op jit(solution)/shard_map/ppermute | solution.py:46
  171.0 7.0 %collective-permute-start.30 = (f32[128,128]{1,0:T(8,128)S(1)}, f32[128,128]{1,0:T(8,128)S(1)}, u32[]{:S(2)}, u32[]{:S(2)}) collective-permute-start(f32[128,128]{1,0:T(8,128)S(1)} %get-tuple-element.66), channel_id=1, source_target_pairs={{0,2},{1,3},{2,0},{3,1},{4,6},{5,7},{6,4},{7,5},{8,34},{9,35},{10,... | collective-permute-start | bytes 196616 | tf_op jit(solution)/shard_map/ppermute | solution.py:46
  175.2 5.5 %collective-permute-start.31 = (f32[128,128]{1,0:T(8,128)S(1)}, f32[128,128]{1,0:T(8,128)S(1)}, u32[]{:S(2)}, u32[]{:S(2)}) collective-permute-start(f32[128,128]{1,0:T(8,128)S(1)} %get-tuple-element.65), channel_id=1, source_target_pairs={{0,6},{1,7},{2,4},{3,5},{4,2},{5,3},{6,0},{7,1},{8,38},{9,39},{10,... | collective-permute-start | bytes 196616 | tf_op jit(solution)/shard_map/ppermute | solution.py:46
  182.5 29.3 %collective-permute-start.32 = (f32[128,256]{1,0:T(8,128)S(1)}, f32[128,256]{1,0:T(8,128)S(1)}, u32[]{:S(2)}, u32[]{:S(2)}) collective-permute-start(f32[128,256]{1,0:T(8,128)S(1)} %get-tuple-element.49), channel_id=1, source_target_pairs={{0,32},{1,33},{2,34},{3,35},{4,36},{5,37},{6,38},{7,39},{8,40},{9,... | collective-permute-start | bytes 393224 | tf_op jit(solution)/shard_map/ppermute | solution.py:46
  186.1 25.7 %collective-permute-start.33 = (f32[128,256]{1,0:T(8,128)S(1)}, f32[128,256]{1,0:T(8,128)S(1)}, u32[]{:S(2)}, u32[]{:S(2)}) collective-permute-start(f32[128,256]{1,0:T(8,128)S(1)} %get-tuple-element.50), channel_id=1, source_target_pairs={{0,64},{1,65},{2,66},{3,67},{4,68},{5,69},{6,70},{7,71},{8,72},{9,... | collective-permute-start | bytes 393224 | tf_op jit(solution)/shard_map/ppermute | solution.py:46
  194.0 17.8 %collective-permute-start.34 = (f32[128,256]{1,0:T(8,128)S(1)}, f32[128,256]{1,0:T(8,128)S(1)}, u32[]{:S(2)}, u32[]{:S(2)}) collective-permute-start(f32[128,256]{1,0:T(8,128)S(1)} %get-tuple-element.51), channel_id=1, source_target_pairs={{0,96},{1,97},{2,98},{3,99},{4,100},{5,101},{6,102},{7,103},{8,104... | collective-permute-start | bytes 393224 | tf_op jit(solution)/shard_map/ppermute | solution.py:46
  194.0 17.8 %all-to-all-start.1 = ((f32[128,1,128]{2,1,0:T(1,128)}), f32[128,1,128]{2,1,0:T(1,128)S(1)}, u32[]{:S(2)}, u32[]{:S(2)}) async-start(f32[128,1,128]{2,1,0:T(1,128)} %get-tuple-element.52), calls=%async_computation.1 | async-start | bytes 131072 | tf_op jit(solution)/shard_map/all_to_all | solution.py:376
  (3 other events, 3.2 us)

commit v2 on v1

--- a/solution.py
+++ b/solution.py
@@ -13,6 +13,7 @@
 SCEN = ("x", "y", "c")
 EPS = 1e-06
 VMEM = 20 * 2**20
+VMEM_LATE = 56 * 2**20
 
 
 def routes(move):
@@ -144,7 +145,7 @@
             b_over[w, 0] = tile(1, v, 0)
 
 
-def gram(lefts, mean, right, at, sums):
+def gram(lefts, mean, right, at, sums, vmem):
     terms = len(lefts)
     high, low = right
     n = high.shape[1]
@@ -188,7 +189,7 @@
         cost_estimate=pl.CostEstimate(
             flops=6 * terms * h * n * n, bytes_accessed=8 * n * n, transcendentals=0
         ),
-        compiler_params=pltpu.CompilerParams(vmem_limit_bytes=VMEM),
+        compiler_params=pltpu.CompilerParams(vmem_limit_bytes=vmem),
     )(at, *args)
     return res[:terms], res[terms:]
 
@@ -208,16 +209,16 @@
 
 
 def combine_body(
-    at_ref, pa, pb, qa, qb, d_got, p_got, q_got, p_own, p_other, q_left, q_right,
+    at_ref, pa, pb, qa, qb, got, p_own, p_other, q_left, q_right,
     norm0, norm1, near0, near1, far0, own_ref, out1, out2, out3, sums_ref, blocks,
     *, scenarios,
 ):
-    c, e, h = at_ref[0], at_ref[1], at_ref[2]
+    c, h = at_ref[0], at_ref[1]
     first = c == 0
     mine = lambda a, b: jnp.where(first, a, b)
     g = qa.shape[0]
     own = [mine(pa[i], pb[1 - i]) + p_own[i] for i in range(2)]
-    other = [mine(p_got[1 - i], p_got[i]) + p_other[i] for i in range(2)]
+    other = [mine(got[1 - i], got[i]) + p_other[i] for i in range(2)]
     left = [
         mine(pa[2], pb[2]),
         mine(own[0], other[0]),
@@ -225,9 +226,9 @@
         mine(other[0], own[0]),
     ]
     right = [
-        d_got[...],
+        got[2],
         mine(own[1], other[1]),
-        q_got[...] + q_right[...],
+        got[3] + q_right[...],
         mine(other[1], own[1]),
     ]
     squares = None
@@ -239,16 +240,15 @@
     all_of = lambda a: jnp.sum(jnp.sum(a, axis=1, keepdims=True), axis=0, keepdims=True)
     frob = all_of(squares)
     n0, n1, m0, m1 = norm0[...], norm1[...], near0[...], near1[...]
-    straight = n0 * m0 + n1 * m1
-    crossed = n0 * m1 + n1 * m0
+    near = n0 * m0 + n1 * m1
     far = jnp.where(h == 0, n0, n1) * far0[...]
-    beta = all_of(n0 * n0 + n1 * n1 + 2.0 * (jnp.where(e == 0, straight, crossed) + far))
+    beta = all_of(n0 * n0 + n1 * n1 + 2.0 * (near + far))
     trace = all_of(n0 + n1)
     lane = lax.broadcasted_iota(jnp.int32, (1, 128), 1)
     row = jnp.where(lane == 0, trace, jnp.where(lane == 1, beta, jnp.where(lane == 2, frob, 0.0)))
     sums_ref[...] = jnp.broadcast_to(row.reshape(1, 1, 128), sums_ref.shape)
     for i, ref in enumerate((own_ref, out1, out2, out3)):
-        ref[...] = blocks[at_ref[3 + i]]
+        ref[...] = blocks[at_ref[2 + i]]
 
 
 def combine(at, arrays, scenarios):
@@ -298,7 +298,8 @@
 
 
 def halve(keep, away, routes_of):
-    total = keep + send(away, routes_of[0])
+    got = send(away, routes_of[0])
+    total = keep + got
     return total[0] + send(total[1], routes_of[1])
 
 
@@ -321,10 +322,7 @@
     order = n * 4
     x, y, c, z = (lax.axis_index(a) for a in AXES)
     first = c == 0
-    low_z = (z < 2).astype(jnp.int32)
-    early_raw = send(lax.dynamic_slice_in_dim(returns, low_z * half, half), TO_Z)
-    late_raw = send(lax.dynamic_slice_in_dim(returns, (1 - low_z) * half, half), TO_Z)
-    far_raw = send(early_raw, TO_Z)
+    near_raw = send(returns, TO_Z)
     sums = to_everyone(jnp.sum(returns, axis=0, keepdims=True), SCEN)
     mean = jnp.sum(sums, axis=0).reshape(1, n) / scenarios
     mean_near = send(mean, TO_Z)
@@ -334,41 +332,44 @@
     ys = [y ^ i for i in turn]
     cols = [2 * (x ^ i) + k for i in turn for k in (c, 1 - c)]
     right = prepare(returns, mean, jnp.stack(cols))
-    near_z = (z + jnp.where(first, 1, 3)) % 4
-    near_early = (near_z < 2).astype(jnp.int32)
-    far_half = 1 - low_z
+    far_half = (z >= 2).astype(jnp.int32)
+    ahead = (z + jnp.where(first, 3, 1)) % 4
+    far_raw = send(lax.dynamic_slice_in_dim(near_raw, jnp.where(ahead >= 2, half, 0), half), TO_Z)
     (norm0, norm1), d_parts = gram(
-        [returns, returns], mean, right, jnp.stack(ys + [0, 0, 1, 1]), None
+        [returns, returns], mean, right, jnp.stack(ys + [0, 0, 1, 1]), None, VMEM
     )
     d_over = from_core(d_parts)
     (near0, near1), p_parts = gram(
-        [early_raw, late_raw],
+        [near_raw, near_raw],
         mean_near,
         right,
-        jnp.stack(ys + [0, near_early, 0, 1 - near_early]),
+        jnp.stack(ys + [0, 0, 1, 1]),
         [d_parts[0], d_over[0], d_parts[1], d_over[1]],
+        VMEM_LATE,
     )
     pa, pb = finish(p_parts)
-    (far0,), q_parts = gram([far_raw], mean_far, right, jnp.stack(ys + [0, far_half]), None)
+    (far0,), q_parts = gram(
+        [far_raw], mean_far, right, jnp.stack(ys + [0, far_half]), None, VMEM_LATE
+    )
     q_over = from_core(q_parts)
     q_keep = [q_parts[i][:2] + q_over[i][:2] for i in range(2)]
     q_away = [q_parts[i][2:] + q_over[i][2:] for i in range(2)]
     q = finish([q_keep[0], q_away[0], q_keep[1], q_away[1]])
 
     mine = lambda a, b: jnp.where(first, a, b)
-    d_got = send(mine(pb[2], pa[2]), OTHER_CORE)
-    p_got = send(mine(pb[:2], pa[:2]), OTHER_CORE)
     p_flip = flip(jnp.stack([pa[0], pb[0], pa[1], pb[1]]))
     p_other = send(p_flip[:2], FLIP_NEAR[0])
     p_own = send(p_flip[2:], FLIP_NEAR[1])
-    q_got = send(mine(q[1], q[0]), OTHER_CORE)
+    got = send(
+        mine(jnp.concatenate([pb, q[1][None]]), jnp.concatenate([pa, q[0][None]])), OTHER_CORE
+    )
     q_flip = flip(jnp.stack(q))
     q_left = send(q_flip[0], FLIP_FAR[0])
     q_right = send(q_flip[1], FLIP_FAR[1])
-    at = jnp.stack([c, near_early, far_half] + [((x ^ i) - z) % 4 for i in range(4)])
+    at = jnp.stack([c, far_half] + [((x ^ i) - z) % 4 for i in range(4)])
     *tiles, sums = combine(
         at,
-        [pa, pb, q[0], q[1], d_got, p_got, q_got, p_own, p_other, q_left, q_right]
+        [pa, pb, q[0], q[1], got, p_own, p_other, q_left, q_right]
         + [norm0, norm1, near0, near1, far0],
         scenarios,
     )

time: 215 us -> 208 us (0.967)
  local copies, waits for them, and re-layouts: 22.5 us -> 13.4 us
  starting transfers between devices: 74.7 us -> 67.4 us
  Pallas kernels: 33.2 us -> 37.5 us
  other arithmetic: 6.19 us -> 9.17 us
    unnamed x28 -> x38, local copies, waits for them, and re-layouts: 14.3 us -> 7.24 us
    ppermute x35 -> x32, starting transfers between devices: 58.6 us -> 52.9 us  [send(): return lax.ppermute(a, AXES, route)]
    pallas_call x3, Pallas kernels: 27.8 us -> 32.3 us  [gram(): pl.pallas_call(functools.partial(gram_body, terms=terms, extra=bool(sums)...]
    add x8, other arithmetic: 0.63 us -> 3.55 us  [halve(): total = keep + got]
    ppermute x35 -> x32, waiting for transfers between devices: 59.9 us -> 61.9 us  [send(): return lax.ppermute(a, AXES, route)]
  transfers between devices with their start and end apart: 37 -> 34, of which waited for: 15 -> 16; matrix products, arithmetic and copies ran while one was open for 4% -> 7% of each run, Pallas kernels for 9% -> 10%
where the time goes in v2:
time: 208 us; the launch traced here: 206 us
  waiting for transfers between devices  78.4 us (38%)
  starting transfers between devices  67.4 us (32%)
  Pallas kernels  37.5 us (18%)
  local copies, waits for them, and re-layouts  13.4 us (6%)
  other arithmetic  9.17 us (4%)
    ppermute x32, waiting for transfers between devices, send(): return lax.ppermute(a, AXES, route)  61.9 us
    ppermute x32, starting transfers between devices, send(): return lax.ppermute(a, AXES, route)  52.9 us
    pallas_call x3, Pallas kernels, gram(): pl.pallas_call(functools.partial(gram_body, terms=terms, extra=bool(sums)...  32.3 us
    all_to_all x1, waiting for transfers between devices, on_device(): sums = lax.all_to_all(sums, AXES, split_axis=0, concat_axis=0, tiled=True)  8.91 us
    all_to_all x1, waiting for transfers between devices, to_everyone(): return lax.all_to_all(copies, axes, split_axis=0, concat_axis=0, tiled=True)  7.6 us
    all_to_all x1, starting transfers between devices, to_everyone(): return lax.all_to_all(copies, axes, split_axis=0, concat_axis=0, tiled=True)  7.32 us
    unnamed x38, local copies, waits for them, and re-layouts  7.24 us
    all_to_all x1, starting transfers between devices, on_device(): sums = lax.all_to_all(sums, AXES, split_axis=0, concat_axis=0, tiled=True)  7.13 us
  transfers between devices with their start and end apart: 34, of which 16 were waited for; matrix products, arithmetic and copies ran while one was open for 7% of the time, Pallas kernels for 10%

profile of v2, /device:TPU:0, one launch (start us, length us, event | category | flops | bytes accessed | tf_op | source)
XLA Modules:
  0.0 206.4 jit_solution(14437417635265735181)
XLA Ops:
  0.0 4.1 %collective-permute-start.1 = (f32[1024,1024]{1,0:T(8,128)}, f32[1024,1024]{1,0:T(8,128)}, u32[]{:S(2)}, u32[]{:S(2)}) collective-permute-start(f32[1024,1024]{1,0:T(8,128)} %refs_3_.1), channel_id=1, source_target_pairs={{0,3},{1,0},{2,1},{3,2},{4,5},{5,6},{6,7},{7,4},{8,11},{9,8},{10,9... | collective-permute-start | bytes 12582920 | tf_op jit(solution)/shard_map/ppermute | solution.py:47
  4.2 2.5 %reduce_sum.18 = f32[1024]{0:T(1024)S(1)} reduce(f32[1024,1024]{1,0:T(8,128)} %refs_3_.1, f32[]{:T(128)} %constant.63.clone.1), dimensions={0}, to_apply=%region_0.0 | reduce | flops 1047552 | bytes 4198404 | tf_op jit(solution)/shard_map/reduce_sum | solution.py:326
  7.4 7.3 %all-to-all-start = ((f32[32,1,1024]{2,1,0:T(1,128)}), f32[32,1,1024]{2,1,0:T(1,128)S(1)}, u32[]{:S(2)}, u32[]{:S(2)}) async-start(f32[32,1,1024]{2,1,0:T(1,128)} %broadcast_in_dim.10), calls=%async_computation | async-start | bytes 262144 | tf_op jit(solution)/shard_map/all_to_all | solution.py:52
  14.9 7.6 %all-to-all-done = f32[32,1,1024]{2,1,0:T(1,128)S(1)} async-done(((f32[32,1,1024]{2,1,0:T(1,128)}), f32[32,1,1024]{2,1,0:T(1,128)S(1)}, u32[]{:S(2)}, u32[]{:S(2)}) %all-to-all-start) | async-done | bytes 131104 | tf_op jit(solution)/shard_map/all_to_all | solution.py:52
  22.7 2.2 %copy-done = f32[1024,1024]{1,0:T(8,128)S(1)} copy-done((f32[1024,1024]{1,0:T(8,128)S(1)}, f32[1024,1024]{1,0:T(8,128)}, u32[]{:S(2)}) %copy-start) | copy-done | bytes 4194328
  24.8 1.7 prepare.1
  26.6 9.6 %shard_map.17 = (f32[512,1]{1,0:T(8,128)S(1)}, f32[512,1]{1,0:T(8,128)S(1)}, f32[4,4,128,128]{3,2,1,0:T(8,128)S(1)}, f32[4,4,128,128]{3,2,1,0:T(8,128)S(1)}, f32...) custom-call(s32[8]{0:T(128)S(1)} %stack.123.at_ref, f32[1,1024]{1,0:T(1,128)S(1)} %bitcast.83, ...), custom_call_target="tpu_custom_call" | custom-call | flops 6442450944 | bytes 8388608 | tf_op jit(solution)/shard_map/pallas_call | solution.py:183
  39.1 11.4 %collective-permute-done.mean_ref = f32[1,1024]{1,0:T(1,128)S(1)} collective-permute-done((f32[1,1024]{1,0:T(1,128)S(1)}, f32[1,1024]{1,0:T(1,128)S(1)}, u32[]{:S(2)}, u32[]{:S(2)}) %collective-permute-start) | collective-permute-done | bytes 4128 | tf_op jit(solution)/shard_map/ppermute | solution.py:47
  51.8 14.2 %shard_map.18 = (f32[512,1]{1,0:T(8,128)}, f32[512,1]{1,0:T(8,128)}, f32[2,4,3,128,128]{4,3,2,1,0:T(8,128)}, f32[2,4,3,128,128]{4,3,2,1,0:T(8,128)}, f32[2,4,3,1...) custom-call(s32[8]{0:T(128)} %copy-done.4, f32[1,1024]{1,0:T(1,128)} %copy-done.18, ...), custom_call_target="tpu_custom_call" | custom-call | flops 6442450944 | bytes 8388608 | tf_op jit(solution)/shard_map/pallas_call | solution.py:183
  66.0 1.6 collective-permute-start.8
  67.6 1.6 collective-permute-start.4
  69.2 3.3 %constant_dynamic-slice_fusion = f32[512,1024]{1,0:T(8,128)} fusion(f32[1024,1024]{1,0:T(8,128)} %collective-permute-done.1.refs_0_.refs_3_, s32[]{:T(128)S(6)} %select_n.52), kind=kLoop, calls=%fused_computation.40 | loop fusion | bytes 4194308 | tf_op jit(solution)/shard_map/dynamic_slice | solution.py:337
  72.5 3.7 %collective-permute-start.13 = (f32[512,1024]{1,0:T(8,128)}, f32[512,1024]{1,0:T(8,128)}, u32[]{:S(2)}, u32[]{:S(2)}) collective-permute-start(f32[512,1024]{1,0:T(8,128)} %constant_dynamic-slice_fusion), channel_id=1, source_target_pairs={{0,3},{1,0},{2,1},{3,2},{4,5},{5,6},{6,7},{7,4},{8,11},{9,8},{10,9... | collective-permute-start | bytes 6291464 | tf_op jit(solution)/shard_map/ppermute | solution.py:47
  76.2 10.7 %collective-permute-done.8 = f32[2,4,3,128,128]{4,3,2,1,0:T(8,128)} collective-permute-done((f32[2,4,3,128,128]{4,3,2,1,0:T(8,128)}, f32[2,4,3,128,128]{4,3,2,1,0:T(8,128)}, u32[]{:S(2)}, u32[]{:S(2)}) %collective-permute-start.8) | collective-permute-done | bytes 1572896 | tf_op jit(solution)/shard_map/ppermute | solution.py:47
  86.8 1.6 add.128
  89.5 2.8 %collective-permute-start.9 = (f32[4,3,128,128]{3,2,1,0:T(8,128)}, f32[4,3,128,128]{3,2,1,0:T(8,128)}, u32[]{:S(2)}, u32[]{:S(2)}) collective-permute-start(f32[4,3,128,128]{3,2,1,0:T(8,128)} %slice_bitcast_fusion), channel_id=1, source_target_pairs={{0,96},{1,97},{2,98},{3,99},{4,36},{5,37},{6,38},{7,39},{8,104},{9... | collective-permute-start | bytes 2359304 | tf_op jit(solution)/shard_map/ppermute | solution.py:47
  92.2 1.2 copy-done.12
  93.4 1.6 add.124
  95.1 3.1 %collective-permute-start.5 = (f32[4,3,128,128]{3,2,1,0:T(8,128)S(1)}, f32[4,3,128,128]{3,2,1,0:T(8,128)}, u32[]{:S(2)}, u32[]{:S(2)}) collective-permute-start(f32[4,3,128,128]{3,2,1,0:T(8,128)S(1)} %slice_bitcast_fusion.2), channel_id=1, source_target_pairs={{0,24},{1,25},{2,26},{3,27},{4,12},{5,13},{6,14},{7,15},{8,16},{9,... | collective-permute-start | bytes 2359304 | tf_op jit(solution)/shard_map/ppermute | solution.py:47
  98.8 2.3 %collective-permute-start.12 = (f32[1,1024]{1,0:T(1,128)S(1)}, f32[1,1024]{1,0:T(1,128)S(1)}, u32[]{:S(2)}, u32[]{:S(2)}) collective-permute-start(f32[1,1024]{1,0:T(1,128)S(1)} %bitcast.85), channel_id=1, source_target_pairs={{0,2},{1,3},{2,0},{3,1},{4,6},{5,7},{6,4},{7,5},{8,10},{9,11},{10,... | collective-permute-start | bytes 12296 | tf_op jit(solution)/shard_map/ppermute | solution.py:47
  101.1 1.8 collective-permute-done.9
  103.0 1.5 fusion
  104.5 1.7 collective-permute-start.10
  106.7 8.4 %shard_map.19 = (f32[512,1]{1,0:T(8,128)}, f32[4,4,128,128]{3,2,1,0:T(8,128)}, f32[4,4,128,128]{3,2,1,0:T(8,128)}, f32[4,4,128,128]{3,2,1,0:T(8,128)}, f32[4,4,128,128]{3,2,1,0:T(8,128)}) custom-call(s32[6]{0:T(128)} %stack.133.at_ref, f32[1,1024]{1,0:T(1,128)} %copy-done.17, f32[512,1024]{1,0:T(8,128)} %collective-permute-done.13.refs_0_, ...), custom_call_target="tpu_custom_call" | custom-call | flops 3221225472 | bytes 8388608 | tf_op jit(solution)/shard_map/pallas_call | solution.py:183
  115.7 1.2 fusion.1
  117.4 2.3 %collective-permute-start.11 = (f32[3,128,128]{2,1,0:T(8,128)S(1)}, f32[3,128,128]{2,1,0:T(8,128)S(1)}, u32[]{:S(2)}, u32[]{:S(2)}) collective-permute-start(f32[3,128,128]{2,1,0:T(8,128)S(1)} %slice_bitcast_fusion.8), channel_id=1, source_target_pairs={{0,24},{1,25},{2,26},{3,27},{4,12},{5,13},{6,14},{7,15},{8,16},{9,... | collective-permute-start | bytes 589832 | tf_op jit(solution)/shard_map/ppermute | solution.py:47
  119.6 5.1 %collective-permute-done.6 = f32[2,3,128,128]{3,2,1,0:T(8,128)S(1)} collective-permute-done((f32[2,3,128,128]{3,2,1,0:T(8,128)S(1)}, f32[2,3,128,128]{3,2,1,0:T(8,128)S(1)}, u32[]{:S(2)}, u32[]{:S(2)}) %collective-permute-start.6) | collective-permute-done | bytes 393248 | tf_op jit(solution)/shard_map/ppermute | solution.py:47
  124.9 2.8 %collective-permute-start.7 = (f32[3,128,128]{2,1,0:T(8,128)S(1)}, f32[3,128,128]{2,1,0:T(8,128)S(1)}, u32[]{:S(2)}, u32[]{:S(2)}) collective-permute-start(f32[3,128,128]{2,1,0:T(8,128)S(1)} %slice_bitcast_fusion.10), channel_id=1, source_target_pairs={{0,96},{1,97},{2,98},{3,99},{4,36},{5,37},{6,38},{7,39},{8,104},{9... | collective-permute-start | bytes 589832 | tf_op jit(solution)/shard_map/ppermute | solution.py:47
  127.7 4.1 %collective-permute-done.7 = f32[3,128,128]{2,1,0:T(8,128)S(1)} collective-permute-done((f32[3,128,128]{2,1,0:T(8,128)S(1)}, f32[3,128,128]{2,1,0:T(8,128)S(1)}, u32[]{:S(2)}, u32[]{:S(2)}) %collective-permute-start.7) | collective-permute-done | bytes 196640 | tf_op jit(solution)/shard_map/ppermute | solution.py:47
  133.0 8.4 %collective-permute-done.15 = f32[2,4,128,128]{3,2,1,0:T(8,128)S(1)} collective-permute-done((f32[2,4,128,128]{3,2,1,0:T(8,128)S(1)}, f32[2,4,128,128]{3,2,1,0:T(8,128)S(1)}, u32[]{:S(2)}, u32[]{:S(2)}) %collective-permute-start.15) | collective-permute-done | bytes 524320 | tf_op jit(solution)/shard_map/ppermute | solution.py:47
  141.5 2.3 %collective-permute-start.16 = (f32[4,128,128]{2,1,0:T(8,128)S(1)}, f32[4,128,128]{2,1,0:T(8,128)S(1)}, u32[]{:S(2)}, u32[]{:S(2)}) collective-permute-start(f32[4,128,128]{2,1,0:T(8,128)S(1)} %slice_bitcast_fusion.6), channel_id=1, source_target_pairs={{0,24},{1,25},{2,26},{3,27},{4,12},{5,13},{6,14},{7,15},{8,16},{9,... | collective-permute-start | bytes 786440 | tf_op jit(solution)/shard_map/ppermute | solution.py:47
  143.9 2.8 %collective-permute-start.21 = (f32[4,128,128]{2,1,0:T(8,128)S(1)}, f32[4,128,128]{2,1,0:T(8,128)S(1)}, u32[]{:S(2)}, u32[]{:S(2)}) collective-permute-start(f32[4,128,128]{2,1,0:T(8,128)S(1)} %slice_bitcast_fusion.4), channel_id=1, source_target_pairs={{0,96},{1,97},{2,98},{3,99},{4,36},{5,37},{6,38},{7,39},{8,104},{9... | collective-permute-start | bytes 786440 | tf_op jit(solution)/shard_map/ppermute | solution.py:47
  147.3 1.9 collective-permute-done.16
  149.3 2.9 %collective-permute-done.21 = f32[4,128,128]{2,1,0:T(8,128)S(1)} collective-permute-done((f32[4,128,128]{2,1,0:T(8,128)S(1)}, f32[4,128,128]{2,1,0:T(8,128)S(1)}, u32[]{:S(2)}, u32[]{:S(2)}) %collective-permute-start.21) | collective-permute-done | bytes 262176 | tf_op jit(solution)/shard_map/ppermute | solution.py:47
  152.4 3.0 %collective-permute-done.17 = f32[2,128,128]{2,1,0:T(8,128)S(1)} collective-permute-done((f32[2,128,128]{2,1,0:T(8,128)S(1)}, f32[2,128,128]{2,1,0:T(8,128)S(1)}, u32[]{:S(2)}, u32[]{:S(2)}) %collective-permute-start.17) | collective-permute-done | bytes 131104 | tf_op jit(solution)/shard_map/ppermute | solution.py:47
  155.5 3.7 %collective-permute-start.18 = (f32[128,128]{1,0:T(8,128)S(1)}, f32[128,128]{1,0:T(8,128)S(1)}, u32[]{:S(2)}, u32[]{:S(2)}) collective-permute-start(f32[128,128]{1,0:T(8,128)S(1)} %slice_bitcast_fusion.16), channel_id=1, source_target_pairs={{0,96},{1,97},{2,98},{3,99},{4,36},{5,37},{6,38},{7,39},{8,104},{9... | collective-permute-start | bytes 196616 | tf_op jit(solution)/shard_map/ppermute | solution.py:47
  159.2 1.8 collective-permute-done.22
  161.1 1.0 collective-permute-done.18
  162.2 4.4 %collective-permute-done.23 = f32[128,128]{1,0:T(8,128)S(1)} collective-permute-done((f32[128,128]{1,0:T(8,128)S(1)}, f32[128,128]{1,0:T(8,128)S(1)}, u32[]{:S(2)}, u32[]{:S(2)}) %collective-permute-start.23) | collective-permute-done | bytes 65568 | tf_op jit(solution)/shard_map/ppermute | solution.py:47
  167.6 4.6 %collective-permute-start.27 = (f32[128,128]{1,0:T(8,128)S(1)}, f32[128,128]{1,0:T(8,128)S(1)}, u32[]{:S(2)}, u32[]{:S(2)}) collective-permute-start(f32[128,128]{1,0:T(8,128)S(1)} %get-tuple-element.60), channel_id=1, source_target_pairs={{0,2},{1,3},{2,0},{3,1},{4,6},{5,7},{6,4},{7,5},{8,34},{9,35},{10,... | collective-permute-start | bytes 196616 | tf_op jit(solution)/shard_map/ppermute | solution.py:47
  172.5 2.5 %collective-permute-done.27.q_left = f32[128,128]{1,0:T(8,128)S(1)} collective-permute-done((f32[128,128]{1,0:T(8,128)S(1)}, f32[128,128]{1,0:T(8,128)S(1)}, u32[]{:S(2)}, u32[]{:S(2)}) %collective-permute-start.27) | collective-permute-done | bytes 65568 | tf_op jit(solution)/shard_map/ppermute | solution.py:47
  175.0 2.7 %collective-permute-done.28.q_right = f32[128,128]{1,0:T(8,128)S(1)} collective-permute-done((f32[128,128]{1,0:T(8,128)S(1)}, f32[128,128]{1,0:T(8,128)S(1)}, u32[]{:S(2)}, u32[]{:S(2)}) %collective-permute-start.28) | collective-permute-done | bytes 65568 | tf_op jit(solution)/shard_map/ppermute | solution.py:47
  177.8 1.7 combine.1
  179.4 1.7 collective-permute-start.29
  181.1 7.5 %collective-permute-start.30 = (f32[128,256]{1,0:T(8,128)S(1)}, f32[128,256]{1,0:T(8,128)S(1)}, u32[]{:S(2)}, u32[]{:S(2)}) collective-permute-start(f32[128,256]{1,0:T(8,128)S(1)} %get-tuple-element.50), channel_id=1, source_target_pairs={{0,64},{1,65},{2,66},{3,67},{4,68},{5,69},{6,70},{7,71},{8,72},{9,... | collective-permute-start | bytes 393224 | tf_op jit(solution)/shard_map/ppermute | solution.py:47
  188.6 7.1 %all-to-all-start.1 = ((f32[128,1,128]{2,1,0:T(1,128)}), f32[128,1,128]{2,1,0:T(1,128)S(1)}, u32[]{:S(2)}, u32[]{:S(2)}) async-start(f32[128,1,128]{2,1,0:T(1,128)} %get-tuple-element.52), calls=%async_computation.1 | async-start | bytes 131072 | tf_op jit(solution)/shard_map/all_to_all | solution.py:377
  195.9 8.9 %all-to-all-done.1.sums_ref = f32[128,1,128]{2,1,0:T(1,128)S(1)} async-done(((f32[128,1,128]{2,1,0:T(1,128)}), f32[128,1,128]{2,1,0:T(1,128)S(1)}, u32[]{:S(2)}, u32[]{:S(2)}) %all-to-all-start.1) | async-done | bytes 65568 | tf_op jit(solution)/shard_map/all_to_all | solution.py:377
  204.8 1.6 shrink.1
  (115 shorter events, 12.1 us)
Async XLA Ops:
  0.0 50.5 %collective-permute-start.1 = (f32[1024,1024]{1,0:T(8,128)}, f32[1024,1024]{1,0:T(8,128)}, u32[]{:S(2)}, u32[]{:S(2)}) collective-permute-start(f32[1024,1024]{1,0:T(8,128)} %refs_3_.1), channel_id=1, source_target_pairs={{0,3},{1,0},{2,1},{3,2},{4,5},{5,6},{6,7},{7,4},{8,11},{9,8},{10,9... | collective-permute-start | bytes 12582920 | tf_op jit(solution)/shard_map/ppermute | solution.py:47
  7.4 15.2 %all-to-all-start = ((f32[32,1,1024]{2,1,0:T(1,128)}), f32[32,1,1024]{2,1,0:T(1,128)S(1)}, u32[]{:S(2)}, u32[]{:S(2)}) async-start(f32[32,1,1024]{2,1,0:T(1,128)} %broadcast_in_dim.10), calls=%async_computation | async-start | bytes 262144 | tf_op jit(solution)/shard_map/all_to_all | solution.py:52
  14.9 11.7 %copy-start.4 = (s32[8]{0:T(128)}, s32[8]{0:T(128)S(1)}, u32[]{:S(2)}) copy-start(s32[8]{0:T(128)S(1)} %stack.123.at_ref) | copy-start | bytes 100
  22.6 2.2 %copy-start = (f32[1024,1024]{1,0:T(8,128)S(1)}, f32[1024,1024]{1,0:T(8,128)}, u32[]{:S(2)}) copy-start(f32[1024,1024]{1,0:T(8,128)} %refs_3_.1) | copy-start | bytes 12582916
  26.6 9.6 %copy-start.5 = (bf16[1024,1024]{1,0:T(8,128)(2,1)}, bf16[1024,1024]{1,0:T(8,128)(2,1)S(1)}, u32[]{:S(2)}) copy-start(bf16[1024,1024]{1,0:T(8,128)(2,1)S(1)} %get-tuple-element.29.refs_1_.refs_4_) | copy-start | bytes 6291460
  26.6 9.6 %copy-start.6 = (bf16[1024,1024]{1,0:T(8,128)(2,1)}, bf16[1024,1024]{1,0:T(8,128)(2,1)S(1)}, u32[]{:S(2)}) copy-start(bf16[1024,1024]{1,0:T(8,128)(2,1)S(1)} %get-tuple-element.30.refs_2_.refs_5_) | copy-start | bytes 6291460
  38.2 12.3 %collective-permute-start.2 = (f32[4,4,128,128]{3,2,1,0:T(8,128)S(1)}, f32[4,4,128,128]{3,2,1,0:T(8,128)S(1)}, u32[]{:S(2)}, u32[]{:S(2)}) collective-permute-start(f32[4,4,128,128]{3,2,1,0:T(8,128)S(1)} %get-tuple-element.32), channel_id=1, source_target_pairs={{0,4},{1,5},{2,6},{3,7},{4,0},{5,1},{6,2},{7,3},{8,12},{9,13},{10,... | collective-permute-start | bytes 3145736 | tf_op jit(solution)/shard_map/ppermute | solution.py:47
  38.3 12.2 %collective-permute-start.3 = (f32[4,4,128,128]{3,2,1,0:T(8,128)S(1)}, f32[4,4,128,128]{3,2,1,0:T(8,128)S(1)}, u32[]{:S(2)}, u32[]{:S(2)}) collective-permute-start(f32[4,4,128,128]{3,2,1,0:T(8,128)S(1)} %get-tuple-element.34), channel_id=1, source_target_pairs={{0,4},{1,5},{2,6},{3,7},{4,0},{5,1},{6,2},{7,3},{8,12},{9,13},{10,... | collective-permute-start | bytes 3145736 | tf_op jit(solution)/shard_map/ppermute | solution.py:47
  38.7 11.8 %collective-permute-start = (f32[1,1024]{1,0:T(1,128)S(1)}, f32[1,1024]{1,0:T(1,128)S(1)}, u32[]{:S(2)}, u32[]{:S(2)}) collective-permute-start(f32[1,1024]{1,0:T(1,128)S(1)} %bitcast.84), channel_id=1, source_target_pairs={{0,3},{1,0},{2,1},{3,2},{4,5},{5,6},{6,7},{7,4},{8,11},{9,8},{10,9... | collective-permute-start | bytes 12296 | tf_op jit(solution)/shard_map/ppermute | solution.py:47
  50.5 1.3 copy-start.16
  66.0 20.8 %collective-permute-start.8 = (f32[2,4,3,128,128]{4,3,2,1,0:T(8,128)}, f32[2,4,3,128,128]{4,3,2,1,0:T(8,128)}, u32[]{:S(2)}, u32[]{:S(2)}) collective-permute-start(f32[2,4,3,128,128]{4,3,2,1,0:T(8,128)} %get-tuple-element.38), channel_id=1, source_target_pairs={{0,32},{1,33},{2,34},{3,35},{4,100},{5,101},{6,102},{7,103},{8,40}... | collective-permute-start | bytes 4718600 | tf_op jit(solution)/shard_map/ppermute | solution.py:47
  67.6 24.6 %collective-permute-start.4 = (f32[2,4,3,128,128]{4,3,2,1,0:T(8,128)}, f32[2,4,3,128,128]{4,3,2,1,0:T(8,128)S(1)}, u32[]{:S(2)}, u32[]{:S(2)}) collective-permute-start(f32[2,4,3,128,128]{4,3,2,1,0:T(8,128)} %get-tuple-element.36), channel_id=1, source_target_pairs={{0,8},{1,9},{2,10},{3,11},{4,28},{5,29},{6,30},{7,31},{8,0},{9,1},... | collective-permute-start | bytes 4718600 | tf_op jit(solution)/shard_map/ppermute | solution.py:47
  69.2 17.7 %copy-start.11 = (f32[2,4,3,128,128]{4,3,2,1,0:T(8,128)S(1)}, f32[2,4,3,128,128]{4,3,2,1,0:T(8,128)}, u32[]{:S(2)}) copy-start(f32[2,4,3,128,128]{4,3,2,1,0:T(8,128)} %get-tuple-element.37) | copy-start | bytes 4718596
  72.5 33.7 %collective-permute-start.13 = (f32[512,1024]{1,0:T(8,128)}, f32[512,1024]{1,0:T(8,128)}, u32[]{:S(2)}, u32[]{:S(2)}) collective-permute-start(f32[512,1024]{1,0:T(8,128)} %constant_dynamic-slice_fusion), channel_id=1, source_target_pairs={{0,3},{1,0},{2,1},{3,2},{4,5},{5,6},{6,7},{7,4},{8,11},{9,8},{10,9... | collective-permute-start | bytes 6291464 | tf_op jit(solution)/shard_map/ppermute | solution.py:47
  88.5 6.6 %copy-start.9 = (f32[2,4,3,128,128]{4,3,2,1,0:T(8,128)}, f32[2,4,3,128,128]{4,3,2,1,0:T(8,128)S(1)}, u32[]{:S(2)}) copy-start(f32[2,4,3,128,128]{4,3,2,1,0:T(8,128)S(1)} %add.128) | copy-start | bytes 4718596
  88.5 4.9 %copy-start.10 = (f32[2,4,3,128,128]{4,3,2,1,0:T(8,128)S(1)}, f32[2,4,3,128,128]{4,3,2,1,0:T(8,128)}, u32[]{:S(2)}) copy-start(f32[2,4,3,128,128]{4,3,2,1,0:T(8,128)} %get-tuple-element.35) | copy-start | bytes 4718596
  89.5 13.5 %collective-permute-start.9 = (f32[4,3,128,128]{3,2,1,0:T(8,128)}, f32[4,3,128,128]{3,2,1,0:T(8,128)}, u32[]{:S(2)}, u32[]{:S(2)}) collective-permute-start(f32[4,3,128,128]{3,2,1,0:T(8,128)} %slice_bitcast_fusion), channel_id=1, source_target_pairs={{0,96},{1,97},{2,98},{3,99},{4,36},{5,37},{6,38},{7,39},{8,104},{9... | collective-permute-start | bytes 2359304 | tf_op jit(solution)/shard_map/ppermute | solution.py:47
  92.2 1.2 copy-start.12
  95.1 20.5 %collective-permute-start.5 = (f32[4,3,128,128]{3,2,1,0:T(8,128)S(1)}, f32[4,3,128,128]{3,2,1,0:T(8,128)}, u32[]{:S(2)}, u32[]{:S(2)}) collective-permute-start(f32[4,3,128,128]{3,2,1,0:T(8,128)S(1)} %slice_bitcast_fusion.2), channel_id=1, source_target_pairs={{0,24},{1,25},{2,26},{3,27},{4,12},{5,13},{6,14},{7,15},{8,16},{9,... | collective-permute-start | bytes 2359304 | tf_op jit(solution)/shard_map/ppermute | solution.py:47
  98.8 7.3 %collective-permute-start.12 = (f32[1,1024]{1,0:T(1,128)S(1)}, f32[1,1024]{1,0:T(1,128)S(1)}, u32[]{:S(2)}, u32[]{:S(2)}) collective-permute-start(f32[1,1024]{1,0:T(1,128)S(1)} %bitcast.85), channel_id=1, source_target_pairs={{0,2},{1,3},{2,0},{3,1},{4,6},{5,7},{6,4},{7,5},{8,10},{9,11},{10,... | collective-permute-start | bytes 12296 | tf_op jit(solution)/shard_map/ppermute | solution.py:47
  104.5 12.8 %collective-permute-start.10 = (f32[2,3,128,128]{3,2,1,0:T(8,128)S(1)}, f32[2,3,128,128]{3,2,1,0:T(8,128)S(1)}, u32[]{:S(2)}, u32[]{:S(2)}) collective-permute-start(f32[2,3,128,128]{3,2,1,0:T(8,128)S(1)} %slice.169), channel_id=1, source_target_pairs={{0,8},{1,9},{2,10},{3,11},{4,28},{5,29},{6,30},{7,31},{8,0},{9,1},... | collective-permute-start | bytes 1179656 | tf_op jit(solution)/shard_map/ppermute | solution.py:47
  115.1 16.7 %collective-permute-start.14 = (f32[4,4,128,128]{3,2,1,0:T(8,128)}, f32[4,4,128,128]{3,2,1,0:T(8,128)S(1)}, u32[]{:S(2)}, u32[]{:S(2)}) collective-permute-start(f32[4,4,128,128]{3,2,1,0:T(8,128)} %get-tuple-element.40), channel_id=1, source_target_pairs={{0,4},{1,5},{2,6},{3,7},{4,0},{5,1},{6,2},{7,3},{8,12},{9,13},{10,... | collective-permute-start | bytes 3145736 | tf_op jit(solution)/shard_map/ppermute | solution.py:47
  115.1 17.5 %collective-permute-start.19 = (f32[4,4,128,128]{3,2,1,0:T(8,128)}, f32[4,4,128,128]{3,2,1,0:T(8,128)S(1)}, u32[]{:S(2)}, u32[]{:S(2)}) collective-permute-start(f32[4,4,128,128]{3,2,1,0:T(8,128)} %get-tuple-element.42), channel_id=1, source_target_pairs={{0,4},{1,5},{2,6},{3,7},{4,0},{5,1},{6,2},{7,3},{8,12},{9,13},{10,... | collective-permute-start | bytes 3145736 | tf_op jit(solution)/shard_map/ppermute | solution.py:47
  116.9 7.9 %collective-permute-start.6 = (f32[2,3,128,128]{3,2,1,0:T(8,128)S(1)}, f32[2,3,128,128]{3,2,1,0:T(8,128)S(1)}, u32[]{:S(2)}, u32[]{:S(2)}) collective-permute-start(f32[2,3,128,128]{3,2,1,0:T(8,128)S(1)} %slice.163), channel_id=1, source_target_pairs={{0,32},{1,33},{2,34},{3,35},{4,100},{5,101},{6,102},{7,103},{8,40}... | collective-permute-start | bytes 1179656 | tf_op jit(solution)/shard_map/ppermute | solution.py:47
  117.4 14.5 %copy-start.14 = (f32[4,4,128,128]{3,2,1,0:T(8,128)S(1)}, f32[4,4,128,128]{3,2,1,0:T(8,128)}, u32[]{:S(2)}) copy-start(f32[4,4,128,128]{3,2,1,0:T(8,128)} %get-tuple-element.39) | copy-start | bytes 3145732
  117.4 10.3 %collective-permute-start.11 = (f32[3,128,128]{2,1,0:T(8,128)S(1)}, f32[3,128,128]{2,1,0:T(8,128)S(1)}, u32[]{:S(2)}, u32[]{:S(2)}) collective-permute-start(f32[3,128,128]{2,1,0:T(8,128)S(1)} %slice_bitcast_fusion.8), channel_id=1, source_target_pairs={{0,24},{1,25},{2,26},{3,27},{4,12},{5,13},{6,14},{7,15},{8,16},{9,... | collective-permute-start | bytes 589832 | tf_op jit(solution)/shard_map/ppermute | solution.py:47
  124.9 7.8 %copy-start.13 = (f32[4,4,128,128]{3,2,1,0:T(8,128)S(1)}, f32[4,4,128,128]{3,2,1,0:T(8,128)}, u32[]{:S(2)}) copy-start(f32[4,4,128,128]{3,2,1,0:T(8,128)} %get-tuple-element.41) | copy-start | bytes 3145732
  124.9 7.0 %collective-permute-start.7 = (f32[3,128,128]{2,1,0:T(8,128)S(1)}, f32[3,128,128]{2,1,0:T(8,128)S(1)}, u32[]{:S(2)}, u32[]{:S(2)}) collective-permute-start(f32[3,128,128]{2,1,0:T(8,128)S(1)} %slice_bitcast_fusion.10), channel_id=1, source_target_pairs={{0,96},{1,97},{2,98},{3,99},{4,36},{5,37},{6,38},{7,39},{8,104},{9... | collective-permute-start | bytes 589832 | tf_op jit(solution)/shard_map/ppermute | solution.py:47
  131.9 9.4 %collective-permute-start.15 = (f32[2,4,128,128]{3,2,1,0:T(8,128)S(1)}, f32[2,4,128,128]{3,2,1,0:T(8,128)S(1)}, u32[]{:S(2)}, u32[]{:S(2)}) collective-permute-start(f32[2,4,128,128]{3,2,1,0:T(8,128)S(1)} %slice_add_fusion.2), channel_id=1, source_target_pairs={{0,8},{1,9},{2,10},{3,11},{4,28},{5,29},{6,30},{7,31},{8,0},{9,1},... | collective-permute-start | bytes 1572872 | tf_op jit(solution)/shard_map/ppermute | solution.py:47
  132.7 11.0 %collective-permute-start.20 = (f32[2,4,128,128]{3,2,1,0:T(8,128)S(1)}, f32[2,4,128,128]{3,2,1,0:T(8,128)S(1)}, u32[]{:S(2)}, u32[]{:S(2)}) collective-permute-start(f32[2,4,128,128]{3,2,1,0:T(8,128)S(1)} %slice_add_fusion), channel_id=1, source_target_pairs={{0,32},{1,33},{2,34},{3,35},{4,100},{5,101},{6,102},{7,103},{8,40}... | collective-permute-start | bytes 1572872 | tf_op jit(solution)/shard_map/ppermute | solution.py:47
  141.5 7.7 %collective-permute-start.16 = (f32[4,128,128]{2,1,0:T(8,128)S(1)}, f32[4,128,128]{2,1,0:T(8,128)S(1)}, u32[]{:S(2)}, u32[]{:S(2)}) collective-permute-start(f32[4,128,128]{2,1,0:T(8,128)S(1)} %slice_bitcast_fusion.6), channel_id=1, source_target_pairs={{0,24},{1,25},{2,26},{3,27},{4,12},{5,13},{6,14},{7,15},{8,16},{9,... | collective-permute-start | bytes 786440 | tf_op jit(solution)/shard_map/ppermute | solution.py:47
  143.9 8.4 %collective-permute-start.21 = (f32[4,128,128]{2,1,0:T(8,128)S(1)}, f32[4,128,128]{2,1,0:T(8,128)S(1)}, u32[]{:S(2)}, u32[]{:S(2)}) collective-permute-start(f32[4,128,128]{2,1,0:T(8,128)S(1)} %slice_bitcast_fusion.4), channel_id=1, source_target_pairs={{0,96},{1,97},{2,98},{3,99},{4,36},{5,37},{6,38},{7,39},{8,104},{9... | collective-permute-start | bytes 786440 | tf_op jit(solution)/shard_map/ppermute | solution.py:47
  146.7 25.8 %collective-permute-start.25 = (f32[2,128,128]{2,1,0:T(8,128)S(1)}, f32[2,128,128]{2,1,0:T(8,128)S(1)}, u32[]{:S(2)}, u32[]{:S(2)}) collective-permute-start(f32[2,128,128]{2,1,0:T(8,128)S(1)} %get-tuple-element.54), channel_id=1, source_target_pairs={{0,5},{1,6},{2,7},{3,4},{4,3},{5,0},{6,1},{7,2},{8,37},{9,38},{10,... | collective-permute-start | bytes 393224 | tf_op jit(solution)/shard_map/ppermute | solution.py:47
  146.8 25.7 %collective-permute-start.26 = (f32[2,128,128]{2,1,0:T(8,128)S(1)}, f32[2,128,128]{2,1,0:T(8,128)S(1)}, u32[]{:S(2)}, u32[]{:S(2)}) collective-permute-start(f32[2,128,128]{2,1,0:T(8,128)S(1)} %get-tuple-element.53), channel_id=1, source_target_pairs={{0,1},{1,2},{2,3},{3,0},{4,7},{5,4},{6,5},{7,6},{8,33},{9,34},{10,... | collective-permute-start | bytes 393224 | tf_op jit(solution)/shard_map/ppermute | solution.py:47
  149.2 6.3 %collective-permute-start.17 = (f32[2,128,128]{2,1,0:T(8,128)S(1)}, f32[2,128,128]{2,1,0:T(8,128)S(1)}, u32[]{:S(2)}, u32[]{:S(2)}) collective-permute-start(f32[2,128,128]{2,1,0:T(8,128)S(1)} %slice.177), channel_id=1, source_target_pairs={{0,32},{1,33},{2,34},{3,35},{4,100},{5,101},{6,102},{7,103},{8,40}... | collective-permute-start | bytes 393224 | tf_op jit(solution)/shard_map/ppermute | solution.py:47
  152.3 25.4 %copy-start.1 = (f32[512,1]{1,0:T(8,128)S(1)}, f32[512,1]{1,0:T(8,128)}, u32[]{:S(2)}) copy-start(f32[512,1]{1,0:T(8,128)} %get-tuple-element.45.near0) | copy-start | bytes 6148
  152.3 25.4 %copy-start.2 = (f32[512,1]{1,0:T(8,128)S(1)}, f32[512,1]{1,0:T(8,128)}, u32[]{:S(2)}) copy-start(f32[512,1]{1,0:T(8,128)} %get-tuple-element.46.near1) | copy-start | bytes 6148
  152.3 25.4 %copy-start.3 = (f32[512,1]{1,0:T(8,128)S(1)}, f32[512,1]{1,0:T(8,128)}, u32[]{:S(2)}) copy-start(f32[512,1]{1,0:T(8,128)} %get-tuple-element.47.far0) | copy-start | bytes 6148
  152.3 8.7 %collective-permute-start.22 = (f32[2,128,128]{2,1,0:T(8,128)S(1)}, f32[2,128,128]{2,1,0:T(8,128)S(1)}, u32[]{:S(2)}, u32[]{:S(2)}) collective-permute-start(f32[2,128,128]{2,1,0:T(8,128)S(1)} %slice.185), channel_id=1, source_target_pairs={{0,8},{1,9},{2,10},{3,11},{4,28},{5,29},{6,30},{7,31},{8,0},{9,1},... | collective-permute-start | bytes 393224 | tf_op jit(solution)/shard_map/ppermute | solution.py:47
  155.5 6.7 %collective-permute-start.18 = (f32[128,128]{1,0:T(8,128)S(1)}, f32[128,128]{1,0:T(8,128)S(1)}, u32[]{:S(2)}, u32[]{:S(2)}) collective-permute-start(f32[128,128]{1,0:T(8,128)S(1)} %slice_bitcast_fusion.16), channel_id=1, source_target_pairs={{0,96},{1,97},{2,98},{3,99},{4,36},{5,37},{6,38},{7,39},{8,104},{9... | collective-permute-start | bytes 196616 | tf_op jit(solution)/shard_map/ppermute | solution.py:47
  161.0 5.6 %collective-permute-start.23 = (f32[128,128]{1,0:T(8,128)S(1)}, f32[128,128]{1,0:T(8,128)S(1)}, u32[]{:S(2)}, u32[]{:S(2)}) collective-permute-start(f32[128,128]{1,0:T(8,128)S(1)} %slice_bitcast_fusion.14), channel_id=1, source_target_pairs={{0,24},{1,25},{2,26},{3,27},{4,12},{5,13},{6,14},{7,15},{8,16},{9,... | collective-permute-start | bytes 196616 | tf_op jit(solution)/shard_map/ppermute | solution.py:47
  166.7 11.1 %collective-permute-start.24 = (f32[4,128,128]{2,1,0:T(8,128)S(1)}, f32[4,128,128]{2,1,0:T(8,128)S(1)}, u32[]{:S(2)}, u32[]{:S(2)}) collective-permute-start(f32[4,128,128]{2,1,0:T(8,128)S(1)} %maximum_select_fusion), channel_id=1, source_target_pairs={{0,4},{1,5},{2,6},{3,7},{4,0},{5,1},{6,2},{7,3},{8,12},{9,13},{10,... | collective-permute-start | bytes 786440 | tf_op jit(solution)/shard_map/ppermute | solution.py:47
  167.6 7.3 %collective-permute-start.27 = (f32[128,128]{1,0:T(8,128)S(1)}, f32[128,128]{1,0:T(8,128)S(1)}, u32[]{:S(2)}, u32[]{:S(2)}) collective-permute-start(f32[128,128]{1,0:T(8,128)S(1)} %get-tuple-element.60), channel_id=1, source_target_pairs={{0,2},{1,3},{2,0},{3,1},{4,6},{5,7},{6,4},{7,5},{8,34},{9,35},{10,... | collective-permute-start | bytes 196616 | tf_op jit(solution)/shard_map/ppermute | solution.py:47
  172.2 5.5 %collective-permute-start.28 = (f32[128,128]{1,0:T(8,128)S(1)}, f32[128,128]{1,0:T(8,128)S(1)}, u32[]{:S(2)}, u32[]{:S(2)}) collective-permute-start(f32[128,128]{1,0:T(8,128)S(1)} %get-tuple-element.59), channel_id=1, source_target_pairs={{0,6},{1,7},{2,4},{3,5},{4,2},{5,3},{6,0},{7,1},{8,38},{9,39},{10,... | collective-permute-start | bytes 196616 | tf_op jit(solution)/shard_map/ppermute | solution.py:47
  179.4 25.4 %collective-permute-start.29 = (f32[128,256]{1,0:T(8,128)S(1)}, f32[128,256]{1,0:T(8,128)S(1)}, u32[]{:S(2)}, u32[]{:S(2)}) collective-permute-start(f32[128,256]{1,0:T(8,128)S(1)} %get-tuple-element.49), channel_id=1, source_target_pairs={{0,32},{1,33},{2,34},{3,35},{4,36},{5,37},{6,38},{7,39},{8,40},{9,... | collective-permute-start | bytes 393224 | tf_op jit(solution)/shard_map/ppermute | solution.py:47
  181.1 23.7 %collective-permute-start.30 = (f32[128,256]{1,0:T(8,128)S(1)}, f32[128,256]{1,0:T(8,128)S(1)}, u32[]{:S(2)}, u32[]{:S(2)}) collective-permute-start(f32[128,256]{1,0:T(8,128)S(1)} %get-tuple-element.50), channel_id=1, source_target_pairs={{0,64},{1,65},{2,66},{3,67},{4,68},{5,69},{6,70},{7,71},{8,72},{9,... | collective-permute-start | bytes 393224 | tf_op jit(solution)/shard_map/ppermute | solution.py:47
  188.6 16.2 %collective-permute-start.31 = (f32[128,256]{1,0:T(8,128)S(1)}, f32[128,256]{1,0:T(8,128)S(1)}, u32[]{:S(2)}, u32[]{:S(2)}) collective-permute-start(f32[128,256]{1,0:T(8,128)S(1)} %get-tuple-element.51), channel_id=1, source_target_pairs={{0,96},{1,97},{2,98},{3,99},{4,100},{5,101},{6,102},{7,103},{8,104... | collective-permute-start | bytes 393224 | tf_op jit(solution)/shard_map/ppermute | solution.py:47
  188.6 16.1 %all-to-all-start.1 = ((f32[128,1,128]{2,1,0:T(1,128)}), f32[128,1,128]{2,1,0:T(1,128)S(1)}, u32[]{:S(2)}, u32[]{:S(2)}) async-start(f32[128,1,128]{2,1,0:T(1,128)} %get-tuple-element.52), calls=%async_computation.1 | async-start | bytes 131072 | tf_op jit(solution)/shard_map/all_to_all | solution.py:377
  (5 other events, 4.2 us)

commit v3 on v2

--- a/solution.py
+++ b/solution.py
@@ -93,13 +93,13 @@
     if extra:
         sums, refs = refs[:4], refs[4:]
     norms, outs = refs[:terms], refs[terms:]
-    dims = (((0,), (0,)), ((), ()))
+    dims = (((1,), (0,)), ((), ()))
     dot = lambda l, r: lax.dot_general(l, r, dims, preferred_element_type=jnp.float32)
     total = None
     for t in range(terms):
         a_ref, high_ref, low_ref = ins[3 * t : 3 * t + 3]
-        a = a_ref[...] - mean_ref[...]
-        norm = jnp.sum(a * a, axis=1, keepdims=True)
+        a = (a_ref[...] - mean_ref[...]).T
+        norm = jnp.sum(a * a, axis=0, keepdims=True)
 
         @pl.when(k == 0)
         def _():
@@ -162,8 +162,8 @@
         args += [left, high, low]
     in_row = pl.BlockSpec((1, 4, g, g), lambda k, at: (k, 0, 0, 0))
     in_col = pl.BlockSpec((4, 1, g, g), lambda k, at: (0, k, 0, 0))
-    shapes = [(h, 1)] * terms
-    outs = [pl.BlockSpec((h, 1), lambda k, at: (0, 0))] * terms
+    shapes = [(1, h)] * terms
+    outs = [pl.BlockSpec((1, h), lambda k, at: (0, 0))] * terms
     if sums:
         specs += [in_row, in_row, in_col, in_col]
         args += sums
@@ -213,7 +213,7 @@
     norm0, norm1, near0, near1, far0, own_ref, out1, out2, out3, sums_ref, blocks,
     *, scenarios,
 ):
-    c, h = at_ref[0], at_ref[1]
+    c, e, h = at_ref[0], at_ref[1], at_ref[2]
     first = c == 0
     mine = lambda a, b: jnp.where(first, a, b)
     g = qa.shape[0]
@@ -240,15 +240,16 @@
     all_of = lambda a: jnp.sum(jnp.sum(a, axis=1, keepdims=True), axis=0, keepdims=True)
     frob = all_of(squares)
     n0, n1, m0, m1 = norm0[...], norm1[...], near0[...], near1[...]
-    near = n0 * m0 + n1 * m1
+    straight = n0 * m0 + n1 * m1
+    crossed = n0 * m1 + n1 * m0
     far = jnp.where(h == 0, n0, n1) * far0[...]
-    beta = all_of(n0 * n0 + n1 * n1 + 2.0 * (near + far))
+    beta = all_of(n0 * n0 + n1 * n1 + 2.0 * (jnp.where(e == 0, straight, crossed) + far))
     trace = all_of(n0 + n1)
     lane = lax.broadcasted_iota(jnp.int32, (1, 128), 1)
     row = jnp.where(lane == 0, trace, jnp.where(lane == 1, beta, jnp.where(lane == 2, frob, 0.0)))
     sums_ref[...] = jnp.broadcast_to(row.reshape(1, 1, 128), sums_ref.shape)
     for i, ref in enumerate((own_ref, out1, out2, out3)):
-        ref[...] = blocks[at_ref[2 + i]]
+        ref[...] = blocks[at_ref[3 + i]]
 
 
 def combine(at, arrays, scenarios):
@@ -322,7 +323,12 @@
     order = n * 4
     x, y, c, z = (lax.axis_index(a) for a in AXES)
     first = c == 0
-    near_raw = send(returns, TO_Z)
+    low_z = (z < 2).astype(jnp.int32)
+    early = lax.dynamic_slice_in_dim(returns, low_z * half, half)
+    early, again = lax.optimization_barrier((early, returns))
+    early_raw = send(early, TO_Z)
+    late_raw = send(lax.dynamic_slice_in_dim(again, (1 - low_z) * half, half), TO_Z)
+    far_raw = send(early_raw, TO_Z)
     sums = to_everyone(jnp.sum(returns, axis=0, keepdims=True), SCEN)
     mean = jnp.sum(sums, axis=0).reshape(1, n) / scenarios
     mean_near = send(mean, TO_Z)
@@ -332,18 +338,18 @@
     ys = [y ^ i for i in turn]
     cols = [2 * (x ^ i) + k for i in turn for k in (c, 1 - c)]
     right = prepare(returns, mean, jnp.stack(cols))
-    far_half = (z >= 2).astype(jnp.int32)
-    ahead = (z + jnp.where(first, 3, 1)) % 4
-    far_raw = send(lax.dynamic_slice_in_dim(near_raw, jnp.where(ahead >= 2, half, 0), half), TO_Z)
+    near_z = (z + jnp.where(first, 1, 3)) % 4
+    near_early = (near_z < 2).astype(jnp.int32)
+    far_half = 1 - low_z
     (norm0, norm1), d_parts = gram(
         [returns, returns], mean, right, jnp.stack(ys + [0, 0, 1, 1]), None, VMEM
     )
     d_over = from_core(d_parts)
     (near0, near1), p_parts = gram(
-        [near_raw, near_raw],
+        [early_raw, late_raw],
         mean_near,
         right,
-        jnp.stack(ys + [0, 0, 1, 1]),
+        jnp.stack(ys + [0, near_early, 0, 1 - near_early]),
         [d_parts[0], d_over[0], d_parts[1], d_over[1]],
         VMEM_LATE,
     )
@@ -366,7 +372,7 @@
     q_flip = flip(jnp.stack(q))
     q_left = send(q_flip[0], FLIP_FAR[0])
     q_right = send(q_flip[1], FLIP_FAR[1])
-    at = jnp.stack([c, far_half] + [((x ^ i) - z) % 4 for i in range(4)])
+    at = jnp.stack([c, near_early, far_half] + [((x ^ i) - z) % 4 for i in range(4)])
     *tiles, sums = combine(
         at,
         [pa, pb, q[0], q[1], got, p_own, p_other, q_left, q_right]

time: 208 us -> 208 us (level)
    unnamed x38 -> x26, local copies, waits for them, and re-layouts: 7.24 us -> 5.35 us
    dynamic_slice x1 -> x2, local copies, waits for them, and re-layouts: 3.28 us -> 4.89 us  [the longest x1 3.16 us: on_device(): lax.dynamic_slice_in_dim(again, (1 - low_z) * half, half)]
    ppermute x32 -> x33, waiting for transfers between devices: 61.9 us -> 62.3 us  [send(): return lax.ppermute(a, AXES, route)]
    ppermute x32 -> x33, starting transfers between devices: 52.9 us -> 53 us  [send(): return lax.ppermute(a, AXES, route)]
  transfers between devices with their start and end apart: 34 -> 35, of which waited for: 16 -> 16; matrix products, arithmetic and copies ran while one was open for 7% -> 7% of each run, Pallas kernels for 10% -> 10%
where the time goes in v3:
time: 208 us; the launch traced here: 207 us
  waiting for transfers between devices  78.8 us (38%)
  starting transfers between devices  67.4 us (32%)
  Pallas kernels  37.7 us (18%)
  local copies, waits for them, and re-layouts  14.7 us (7%)
  other arithmetic  7.58 us (4%)
    ppermute x33, waiting for transfers between devices, send(): return lax.ppermute(a, AXES, route)  62.3 us
    ppermute x33, starting transfers between devices, send(): return lax.ppermute(a, AXES, route)  53 us
    pallas_call x3, Pallas kernels, gram(): pl.pallas_call(functools.partial(gram_body, terms=terms, extra=bool(sums)...  32.7 us
    all_to_all x1, waiting for transfers between devices, on_device(): sums = lax.all_to_all(sums, AXES, split_axis=0, concat_axis=0, tiled=True)  8.91 us
    all_to_all x1, waiting for transfers between devices, to_everyone(): return lax.all_to_all(copies, axes, split_axis=0, concat_axis=0, tiled=True)  7.6 us
    all_to_all x1, starting transfers between devices, to_everyone(): return lax.all_to_all(copies, axes, split_axis=0, concat_axis=0, tiled=True)  7.32 us
    all_to_all x1, starting transfers between devices, on_device(): sums = lax.all_to_all(sums, AXES, split_axis=0, concat_axis=0, tiled=True)  7.1 us
    unnamed x26, local copies, waits for them, and re-layouts  5.35 us
  transfers between devices with their start and end apart: 35, of which 16 were waited for; matrix products, arithmetic and copies ran while one was open for 7% of the time, Pallas kernels for 10%

profile of v3, /device:TPU:0, one launch (start us, length us, event | category | flops | bytes accessed | tf_op | source)
XLA Modules:
  0.0 206.7 jit_solution(15631342039631836133)
XLA Ops:
  0.0 1.7 constant_dynamic-slice_fusion.1
  1.7 4.2 %collective-permute-start.1 = (f32[512,1024]{1,0:T(8,128)S(1)}, f32[512,1024]{1,0:T(8,128)}, u32[]{:S(2)}, u32[]{:S(2)}) collective-permute-start(f32[512,1024]{1,0:T(8,128)S(1)} %constant_dynamic-slice_fusion.1), channel_id=1, source_target_pairs={{0,3},{1,0},{2,1},{3,2},{4,5},{5,6},{6,7},{7,4},{8,11},{9,8},{10,9... | collective-permute-start | bytes 6291464 | tf_op jit(solution)/shard_map/ppermute | solution.py:47
  5.9 3.2 %constant_dynamic-slice_fusion = f32[512,1024]{1,0:T(8,128)} fusion(f32[1024,1024]{1,0:T(8,128)} %refs_3_.1, s32[]{:T(128)S(6)} %select_n.52), kind=kLoop, calls=%fused_computation.40 | loop fusion | bytes 4194308 | tf_op jit(solution)/shard_map/dynamic_slice | solution.py:330
  9.5 2.5 %reduce_sum.18 = f32[1024]{0:T(1024)S(1)} reduce(f32[1024,1024]{1,0:T(8,128)} %refs_3_.1, f32[]{:T(128)} %constant.65.clone.1), dimensions={0}, to_apply=%region_0.0 | reduce | flops 1047552 | bytes 4198404 | tf_op jit(solution)/shard_map/reduce_sum | solution.py:332
  12.7 7.3 %all-to-all-start = ((f32[32,1,1024]{2,1,0:T(1,128)}), f32[32,1,1024]{2,1,0:T(1,128)S(1)}, u32[]{:S(2)}, u32[]{:S(2)}) async-start(f32[32,1,1024]{2,1,0:T(1,128)} %broadcast_in_dim.10), calls=%async_computation | async-start | bytes 262144 | tf_op jit(solution)/shard_map/all_to_all | solution.py:52
  20.3 7.6 %all-to-all-done = f32[32,1,1024]{2,1,0:T(1,128)S(1)} async-done(((f32[32,1,1024]{2,1,0:T(1,128)}), f32[32,1,1024]{2,1,0:T(1,128)S(1)}, u32[]{:S(2)}, u32[]{:S(2)}) %all-to-all-start) | async-done | bytes 131104 | tf_op jit(solution)/shard_map/all_to_all | solution.py:52
  28.0 2.2 %copy-done = f32[1024,1024]{1,0:T(8,128)S(1)} copy-done((f32[1024,1024]{1,0:T(8,128)S(1)}, f32[1024,1024]{1,0:T(8,128)}, u32[]{:S(2)}) %copy-start) | copy-done | bytes 4194328
  30.2 1.7 prepare.1
  31.9 10.2 %shard_map.17 = (f32[1,512]{1,0:T(1,128)S(1)}, f32[1,512]{1,0:T(1,128)S(1)}, f32[4,4,128,128]{3,2,1,0:T(8,128)S(1)}, f32[4,4,128,128]{3,2,1,0:T(8,128)S(1)}, f32...) custom-call(s32[8]{0:T(128)S(1)} %stack.140.at_ref, f32[1,1024]{1,0:T(1,128)S(1)} %bitcast.85, ...), custom_call_target="tpu_custom_call" | custom-call | flops 6442450944 | bytes 8388608 | tf_op jit(solution)/shard_map/pallas_call | solution.py:183
  45.3 6.8 %collective-permute-done.mean_ref = f32[1,1024]{1,0:T(1,128)S(1)} collective-permute-done((f32[1,1024]{1,0:T(1,128)S(1)}, f32[1,1024]{1,0:T(1,128)S(1)}, u32[]{:S(2)}, u32[]{:S(2)}) %collective-permute-start) | collective-permute-done | bytes 4128 | tf_op jit(solution)/shard_map/ppermute | solution.py:47
  52.7 14.0 %shard_map.18 = (f32[1,512]{1,0:T(1,128)}, f32[1,512]{1,0:T(1,128)}, f32[2,4,3,128,128]{4,3,2,1,0:T(8,128)}, f32[2,4,3,128,128]{4,3,2,1,0:T(8,128)}, f32[2,4,3,1...) custom-call(s32[8]{0:T(128)} %stack.130.at_ref, f32[1,1024]{1,0:T(1,128)} %copy-done.11, ...), custom_call_target="tpu_custom_call" | custom-call | flops 6442450944 | bytes 8388608 | tf_op jit(solution)/shard_map/pallas_call | solution.py:183
  66.7 1.6 collective-permute-start.9
  68.3 1.6 collective-permute-start.5
  69.8 3.7 %collective-permute-start.14 = (f32[512,1024]{1,0:T(8,128)}, f32[512,1024]{1,0:T(8,128)}, u32[]{:S(2)}, u32[]{:S(2)}) collective-permute-start(f32[512,1024]{1,0:T(8,128)} %collective-permute-done.1.refs_0_), channel_id=1, source_target_pairs={{0,3},{1,0},{2,1},{3,2},{4,5},{5,6},{6,7},{7,4},{8,11},{9,8},{10,9... | collective-permute-start | bytes 6291464 | tf_op jit(solution)/shard_map/ppermute | solution.py:47
  73.5 13.9 %collective-permute-done.9 = f32[2,4,3,128,128]{4,3,2,1,0:T(8,128)S(1)} collective-permute-done((f32[2,4,3,128,128]{4,3,2,1,0:T(8,128)}, f32[2,4,3,128,128]{4,3,2,1,0:T(8,128)S(1)}, u32[]{:S(2)}, u32[]{:S(2)}) %collective-permute-start.9) | collective-permute-done | bytes 1572896 | tf_op jit(solution)/shard_map/ppermute | solution.py:47
  87.4 1.8 add.134
  89.2 1.0 slice_bitcast_fusion
  90.2 2.8 %collective-permute-start.10 = (f32[4,3,128,128]{3,2,1,0:T(8,128)}, f32[4,3,128,128]{3,2,1,0:T(8,128)}, u32[]{:S(2)}, u32[]{:S(2)}) collective-permute-start(f32[4,3,128,128]{3,2,1,0:T(8,128)} %slice_bitcast_fusion), channel_id=1, source_target_pairs={{0,96},{1,97},{2,98},{3,99},{4,36},{5,37},{6,38},{7,39},{8,104},{9... | collective-permute-start | bytes 2359304 | tf_op jit(solution)/shard_map/ppermute | solution.py:47
  94.0 3.0 %collective-permute-start.6 = (f32[4,3,128,128]{3,2,1,0:T(8,128)}, f32[4,3,128,128]{3,2,1,0:T(8,128)}, u32[]{:S(2)}, u32[]{:S(2)}) collective-permute-start(f32[4,3,128,128]{3,2,1,0:T(8,128)} %slice_bitcast_fusion.2), channel_id=1, source_target_pairs={{0,24},{1,25},{2,26},{3,27},{4,12},{5,13},{6,14},{7,15},{8,16},{9,... | collective-permute-start | bytes 2359304 | tf_op jit(solution)/shard_map/ppermute | solution.py:47
  97.7 2.3 %collective-permute-start.13 = (f32[1,1024]{1,0:T(1,128)S(1)}, f32[1,1024]{1,0:T(1,128)S(1)}, u32[]{:S(2)}, u32[]{:S(2)}) collective-permute-start(f32[1,1024]{1,0:T(1,128)S(1)} %bitcast.87), channel_id=1, source_target_pairs={{0,2},{1,3},{2,0},{3,1},{4,6},{5,7},{6,4},{7,5},{8,10},{9,11},{10,... | collective-permute-start | bytes 12296 | tf_op jit(solution)/shard_map/ppermute | solution.py:47
  100.0 3.6 %collective-permute-done.10 = f32[4,3,128,128]{3,2,1,0:T(8,128)} collective-permute-done((f32[4,3,128,128]{3,2,1,0:T(8,128)}, f32[4,3,128,128]{3,2,1,0:T(8,128)}, u32[]{:S(2)}, u32[]{:S(2)}) %collective-permute-start.10) | collective-permute-done | bytes 786464 | tf_op jit(solution)/shard_map/ppermute | solution.py:47
  103.7 1.2 fusion
  105.0 1.7 collective-permute-start.11
  107.2 8.5 %shard_map.19 = (f32[1,512]{1,0:T(1,128)}, f32[4,4,128,128]{3,2,1,0:T(8,128)}, f32[4,4,128,128]{3,2,1,0:T(8,128)}, f32[4,4,128,128]{3,2,1,0:T(8,128)}, f32[4,4,128,128]{3,2,1,0:T(8,128)}) custom-call(s32[6]{0:T(128)} %stack.141.at_ref, f32[1,1024]{1,0:T(1,128)} %copy-done.12, f32[512,1024]{1,0:T(8,128)} %collective-permute-done.14.refs_0_, ...), custom_call_target="tpu_custom_call" | custom-call | flops 3221225472 | bytes 8388608 | tf_op jit(solution)/shard_map/pallas_call | solution.py:183
  116.2 1.2 fusion.1
  117.9 2.3 %collective-permute-start.12 = (f32[3,128,128]{2,1,0:T(8,128)S(1)}, f32[3,128,128]{2,1,0:T(8,128)S(1)}, u32[]{:S(2)}, u32[]{:S(2)}) collective-permute-start(f32[3,128,128]{2,1,0:T(8,128)S(1)} %slice_bitcast_fusion.8), channel_id=1, source_target_pairs={{0,24},{1,25},{2,26},{3,27},{4,12},{5,13},{6,14},{7,15},{8,16},{9,... | collective-permute-start | bytes 589832 | tf_op jit(solution)/shard_map/ppermute | solution.py:47
  120.2 5.2 %collective-permute-done.7 = f32[2,3,128,128]{3,2,1,0:T(8,128)S(1)} collective-permute-done((f32[2,3,128,128]{3,2,1,0:T(8,128)S(1)}, f32[2,3,128,128]{3,2,1,0:T(8,128)S(1)}, u32[]{:S(2)}, u32[]{:S(2)}) %collective-permute-start.7) | collective-permute-done | bytes 393248 | tf_op jit(solution)/shard_map/ppermute | solution.py:47
  125.4 3.0 %collective-permute-start.8 = (f32[3,128,128]{2,1,0:T(8,128)S(1)}, f32[3,128,128]{2,1,0:T(8,128)S(1)}, u32[]{:S(2)}, u32[]{:S(2)}) collective-permute-start(f32[3,128,128]{2,1,0:T(8,128)S(1)} %slice_bitcast_fusion.10), channel_id=1, source_target_pairs={{0,96},{1,97},{2,98},{3,99},{4,36},{5,37},{6,38},{7,39},{8,104},{9... | collective-permute-start | bytes 589832 | tf_op jit(solution)/shard_map/ppermute | solution.py:47
  128.5 4.1 %collective-permute-done.8 = f32[3,128,128]{2,1,0:T(8,128)S(1)} collective-permute-done((f32[3,128,128]{2,1,0:T(8,128)S(1)}, f32[3,128,128]{2,1,0:T(8,128)S(1)}, u32[]{:S(2)}, u32[]{:S(2)}) %collective-permute-start.8) | collective-permute-done | bytes 196640 | tf_op jit(solution)/shard_map/ppermute | solution.py:47
  133.6 8.4 %collective-permute-done.16 = f32[2,4,128,128]{3,2,1,0:T(8,128)S(1)} collective-permute-done((f32[2,4,128,128]{3,2,1,0:T(8,128)S(1)}, f32[2,4,128,128]{3,2,1,0:T(8,128)S(1)}, u32[]{:S(2)}, u32[]{:S(2)}) %collective-permute-start.16) | collective-permute-done | bytes 524320 | tf_op jit(solution)/shard_map/ppermute | solution.py:47
  142.1 2.3 %collective-permute-start.17 = (f32[4,128,128]{2,1,0:T(8,128)S(1)}, f32[4,128,128]{2,1,0:T(8,128)S(1)}, u32[]{:S(2)}, u32[]{:S(2)}) collective-permute-start(f32[4,128,128]{2,1,0:T(8,128)S(1)} %slice_bitcast_fusion.6), channel_id=1, source_target_pairs={{0,24},{1,25},{2,26},{3,27},{4,12},{5,13},{6,14},{7,15},{8,16},{9,... | collective-permute-start | bytes 786440 | tf_op jit(solution)/shard_map/ppermute | solution.py:47
  144.4 2.8 %collective-permute-start.22 = (f32[4,128,128]{2,1,0:T(8,128)S(1)}, f32[4,128,128]{2,1,0:T(8,128)S(1)}, u32[]{:S(2)}, u32[]{:S(2)}) collective-permute-start(f32[4,128,128]{2,1,0:T(8,128)S(1)} %slice_bitcast_fusion.4), channel_id=1, source_target_pairs={{0,96},{1,97},{2,98},{3,99},{4,36},{5,37},{6,38},{7,39},{8,104},{9... | collective-permute-start | bytes 786440 | tf_op jit(solution)/shard_map/ppermute | solution.py:47
  147.8 1.9 collective-permute-done.17
  149.9 2.9 %collective-permute-done.22 = f32[4,128,128]{2,1,0:T(8,128)S(1)} collective-permute-done((f32[4,128,128]{2,1,0:T(8,128)S(1)}, f32[4,128,128]{2,1,0:T(8,128)S(1)}, u32[]{:S(2)}, u32[]{:S(2)}) %collective-permute-start.22) | collective-permute-done | bytes 262176 | tf_op jit(solution)/shard_map/ppermute | solution.py:47
  153.0 3.1 %collective-permute-done.18 = f32[2,128,128]{2,1,0:T(8,128)S(1)} collective-permute-done((f32[2,128,128]{2,1,0:T(8,128)S(1)}, f32[2,128,128]{2,1,0:T(8,128)S(1)}, u32[]{:S(2)}, u32[]{:S(2)}) %collective-permute-start.18) | collective-permute-done | bytes 131104 | tf_op jit(solution)/shard_map/ppermute | solution.py:47
  156.1 3.7 %collective-permute-start.19 = (f32[128,128]{1,0:T(8,128)S(1)}, f32[128,128]{1,0:T(8,128)S(1)}, u32[]{:S(2)}, u32[]{:S(2)}) collective-permute-start(f32[128,128]{1,0:T(8,128)S(1)} %slice_bitcast_fusion.16), channel_id=1, source_target_pairs={{0,96},{1,97},{2,98},{3,99},{4,36},{5,37},{6,38},{7,39},{8,104},{9... | collective-permute-start | bytes 196616 | tf_op jit(solution)/shard_map/ppermute | solution.py:47
  159.8 1.8 collective-permute-done.23
  161.7 1.0 collective-permute-done.19
  162.7 4.4 %collective-permute-done.24 = f32[128,128]{1,0:T(8,128)S(1)} collective-permute-done((f32[128,128]{1,0:T(8,128)S(1)}, f32[128,128]{1,0:T(8,128)S(1)}, u32[]{:S(2)}, u32[]{:S(2)}) %collective-permute-start.24) | collective-permute-done | bytes 65568 | tf_op jit(solution)/shard_map/ppermute | solution.py:47
  168.2 4.6 %collective-permute-start.28 = (f32[128,128]{1,0:T(8,128)S(1)}, f32[128,128]{1,0:T(8,128)S(1)}, u32[]{:S(2)}, u32[]{:S(2)}) collective-permute-start(f32[128,128]{1,0:T(8,128)S(1)} %get-tuple-element.64), channel_id=1, source_target_pairs={{0,2},{1,3},{2,0},{3,1},{4,6},{5,7},{6,4},{7,5},{8,34},{9,35},{10,... | collective-permute-start | bytes 196616 | tf_op jit(solution)/shard_map/ppermute | solution.py:47
  173.1 2.5 %collective-permute-done.28.q_left = f32[128,128]{1,0:T(8,128)S(1)} collective-permute-done((f32[128,128]{1,0:T(8,128)S(1)}, f32[128,128]{1,0:T(8,128)S(1)}, u32[]{:S(2)}, u32[]{:S(2)}) %collective-permute-start.28) | collective-permute-done | bytes 65568 | tf_op jit(solution)/shard_map/ppermute | solution.py:47
  175.5 2.7 %collective-permute-done.29.q_right = f32[128,128]{1,0:T(8,128)S(1)} collective-permute-done((f32[128,128]{1,0:T(8,128)S(1)}, f32[128,128]{1,0:T(8,128)S(1)}, u32[]{:S(2)}, u32[]{:S(2)}) %collective-permute-start.29) | collective-permute-done | bytes 65568 | tf_op jit(solution)/shard_map/ppermute | solution.py:47
  178.3 1.4 combine.1
  179.7 1.7 collective-permute-start.30
  181.4 7.5 %collective-permute-start.31 = (f32[128,256]{1,0:T(8,128)S(1)}, f32[128,256]{1,0:T(8,128)S(1)}, u32[]{:S(2)}, u32[]{:S(2)}) collective-permute-start(f32[128,256]{1,0:T(8,128)S(1)} %get-tuple-element.54), channel_id=1, source_target_pairs={{0,64},{1,65},{2,66},{3,67},{4,68},{5,69},{6,70},{7,71},{8,72},{9,... | collective-permute-start | bytes 393224 | tf_op jit(solution)/shard_map/ppermute | solution.py:47
  188.9 7.1 %all-to-all-start.1 = ((f32[128,1,128]{2,1,0:T(1,128)}), f32[128,1,128]{2,1,0:T(1,128)S(1)}, u32[]{:S(2)}, u32[]{:S(2)}) async-start(f32[128,1,128]{2,1,0:T(1,128)} %get-tuple-element.56), calls=%async_computation.1 | async-start | bytes 131072 | tf_op jit(solution)/shard_map/all_to_all | solution.py:383
  196.1 8.9 %all-to-all-done.1.sums_ref = f32[128,1,128]{2,1,0:T(1,128)S(1)} async-done(((f32[128,1,128]{2,1,0:T(1,128)}), f32[128,1,128]{2,1,0:T(1,128)S(1)}, u32[]{:S(2)}, u32[]{:S(2)}) %all-to-all-start.1) | async-done | bytes 65568 | tf_op jit(solution)/shard_map/all_to_all | solution.py:383
  205.0 1.7 shrink.1
  (107 shorter events, 12.1 us)
Async XLA Ops:
  1.7 50.4 %collective-permute-start.1 = (f32[512,1024]{1,0:T(8,128)S(1)}, f32[512,1024]{1,0:T(8,128)}, u32[]{:S(2)}, u32[]{:S(2)}) collective-permute-start(f32[512,1024]{1,0:T(8,128)S(1)} %constant_dynamic-slice_fusion.1), channel_id=1, source_target_pairs={{0,3},{1,0},{2,1},{3,2},{4,5},{5,6},{6,7},{7,4},{8,11},{9,8},{10,9... | collective-permute-start | bytes 6291464 | tf_op jit(solution)/shard_map/ppermute | solution.py:47
  9.1 43.0 %collective-permute-start.2 = (f32[512,1024]{1,0:T(8,128)}, f32[512,1024]{1,0:T(8,128)}, u32[]{:S(2)}, u32[]{:S(2)}) collective-permute-start(f32[512,1024]{1,0:T(8,128)} %constant_dynamic-slice_fusion), channel_id=1, source_target_pairs={{0,3},{1,0},{2,1},{3,2},{4,5},{5,6},{6,7},{7,4},{8,11},{9,8},{10,9... | collective-permute-start | bytes 6291464 | tf_op jit(solution)/shard_map/ppermute | solution.py:47
  12.7 15.2 %all-to-all-start = ((f32[32,1,1024]{2,1,0:T(1,128)}), f32[32,1,1024]{2,1,0:T(1,128)S(1)}, u32[]{:S(2)}, u32[]{:S(2)}) async-start(f32[32,1,1024]{2,1,0:T(1,128)} %broadcast_in_dim.10), calls=%async_computation | async-start | bytes 262144 | tf_op jit(solution)/shard_map/all_to_all | solution.py:52
  28.0 2.2 %copy-start = (f32[1024,1024]{1,0:T(8,128)S(1)}, f32[1024,1024]{1,0:T(8,128)}, u32[]{:S(2)}) copy-start(f32[1024,1024]{1,0:T(8,128)} %refs_3_.1) | copy-start | bytes 12582916
  31.9 10.2 %copy-start.4 = (bf16[1024,1024]{1,0:T(8,128)(2,1)}, bf16[1024,1024]{1,0:T(8,128)(2,1)S(1)}, u32[]{:S(2)}) copy-start(bf16[1024,1024]{1,0:T(8,128)(2,1)S(1)} %get-tuple-element.32.refs_1_.refs_4_) | copy-start | bytes 6291460
  31.9 10.2 %copy-start.5 = (bf16[1024,1024]{1,0:T(8,128)(2,1)}, bf16[1024,1024]{1,0:T(8,128)(2,1)S(1)}, u32[]{:S(2)}) copy-start(bf16[1024,1024]{1,0:T(8,128)(2,1)S(1)} %get-tuple-element.33.refs_2_.refs_5_) | copy-start | bytes 6291460
  42.1 1.0 copy-start.6
  43.1 1.0 copy-start.7
  44.1 8.0 %collective-permute-start.3 = (f32[4,4,128,128]{3,2,1,0:T(8,128)}, f32[4,4,128,128]{3,2,1,0:T(8,128)}, u32[]{:S(2)}, u32[]{:S(2)}) collective-permute-start(f32[4,4,128,128]{3,2,1,0:T(8,128)} %get-tuple-element.36), channel_id=1, source_target_pairs={{0,4},{1,5},{2,6},{3,7},{4,0},{5,1},{6,2},{7,3},{8,12},{9,13},{10,... | collective-permute-start | bytes 3145736 | tf_op jit(solution)/shard_map/ppermute | solution.py:47
  44.2 7.9 %collective-permute-start.4 = (f32[4,4,128,128]{3,2,1,0:T(8,128)S(1)}, f32[4,4,128,128]{3,2,1,0:T(8,128)}, u32[]{:S(2)}, u32[]{:S(2)}) collective-permute-start(f32[4,4,128,128]{3,2,1,0:T(8,128)S(1)} %get-tuple-element.38), channel_id=1, source_target_pairs={{0,4},{1,5},{2,6},{3,7},{4,0},{5,1},{6,2},{7,3},{8,12},{9,13},{10,... | collective-permute-start | bytes 3145736 | tf_op jit(solution)/shard_map/ppermute | solution.py:47
  44.6 7.5 %collective-permute-start = (f32[1,1024]{1,0:T(1,128)S(1)}, f32[1,1024]{1,0:T(1,128)S(1)}, u32[]{:S(2)}, u32[]{:S(2)}) collective-permute-start(f32[1,1024]{1,0:T(1,128)S(1)} %bitcast.86), channel_id=1, source_target_pairs={{0,3},{1,0},{2,1},{3,2},{4,5},{5,6},{6,7},{7,4},{8,11},{9,8},{10,9... | collective-permute-start | bytes 12296 | tf_op jit(solution)/shard_map/ppermute | solution.py:47
  52.1 0.6 copy-start.11
  66.7 20.7 %collective-permute-start.9 = (f32[2,4,3,128,128]{4,3,2,1,0:T(8,128)}, f32[2,4,3,128,128]{4,3,2,1,0:T(8,128)S(1)}, u32[]{:S(2)}, u32[]{:S(2)}) collective-permute-start(f32[2,4,3,128,128]{4,3,2,1,0:T(8,128)} %get-tuple-element.42), channel_id=1, source_target_pairs={{0,32},{1,33},{2,34},{3,35},{4,100},{5,101},{6,102},{7,103},{8,40}... | collective-permute-start | bytes 4718600 | tf_op jit(solution)/shard_map/ppermute | solution.py:47
  68.3 24.7 %collective-permute-start.5 = (f32[2,4,3,128,128]{4,3,2,1,0:T(8,128)}, f32[2,4,3,128,128]{4,3,2,1,0:T(8,128)S(1)}, u32[]{:S(2)}, u32[]{:S(2)}) collective-permute-start(f32[2,4,3,128,128]{4,3,2,1,0:T(8,128)} %get-tuple-element.40), channel_id=1, source_target_pairs={{0,8},{1,9},{2,10},{3,11},{4,28},{5,29},{6,30},{7,31},{8,0},{9,1},... | collective-permute-start | bytes 4718600 | tf_op jit(solution)/shard_map/ppermute | solution.py:47
  69.8 36.8 %collective-permute-start.14 = (f32[512,1024]{1,0:T(8,128)}, f32[512,1024]{1,0:T(8,128)}, u32[]{:S(2)}, u32[]{:S(2)}) collective-permute-start(f32[512,1024]{1,0:T(8,128)} %collective-permute-done.1.refs_0_), channel_id=1, source_target_pairs={{0,3},{1,0},{2,1},{3,2},{4,5},{5,6},{6,7},{7,4},{8,11},{9,8},{10,9... | collective-permute-start | bytes 6291464 | tf_op jit(solution)/shard_map/ppermute | solution.py:47
  87.4 5.5 %copy-start.8 = (f32[2,4,3,128,128]{4,3,2,1,0:T(8,128)S(1)}, f32[2,4,3,128,128]{4,3,2,1,0:T(8,128)}, u32[]{:S(2)}) copy-start(f32[2,4,3,128,128]{4,3,2,1,0:T(8,128)} %get-tuple-element.39) | copy-start | bytes 4718596
  90.2 13.5 %collective-permute-start.10 = (f32[4,3,128,128]{3,2,1,0:T(8,128)}, f32[4,3,128,128]{3,2,1,0:T(8,128)}, u32[]{:S(2)}, u32[]{:S(2)}) collective-permute-start(f32[4,3,128,128]{3,2,1,0:T(8,128)} %slice_bitcast_fusion), channel_id=1, source_target_pairs={{0,96},{1,97},{2,98},{3,99},{4,36},{5,37},{6,38},{7,39},{8,104},{9... | collective-permute-start | bytes 2359304 | tf_op jit(solution)/shard_map/ppermute | solution.py:47
  94.0 22.2 %collective-permute-start.6 = (f32[4,3,128,128]{3,2,1,0:T(8,128)}, f32[4,3,128,128]{3,2,1,0:T(8,128)}, u32[]{:S(2)}, u32[]{:S(2)}) collective-permute-start(f32[4,3,128,128]{3,2,1,0:T(8,128)} %slice_bitcast_fusion.2), channel_id=1, source_target_pairs={{0,24},{1,25},{2,26},{3,27},{4,12},{5,13},{6,14},{7,15},{8,16},{9,... | collective-permute-start | bytes 2359304 | tf_op jit(solution)/shard_map/ppermute | solution.py:47
  97.7 8.9 %collective-permute-start.13 = (f32[1,1024]{1,0:T(1,128)S(1)}, f32[1,1024]{1,0:T(1,128)S(1)}, u32[]{:S(2)}, u32[]{:S(2)}) collective-permute-start(f32[1,1024]{1,0:T(1,128)S(1)} %bitcast.87), channel_id=1, source_target_pairs={{0,2},{1,3},{2,0},{3,1},{4,6},{5,7},{6,4},{7,5},{8,10},{9,11},{10,... | collective-permute-start | bytes 12296 | tf_op jit(solution)/shard_map/ppermute | solution.py:47
  105.0 12.9 %collective-permute-start.11 = (f32[2,3,128,128]{3,2,1,0:T(8,128)S(1)}, f32[2,3,128,128]{3,2,1,0:T(8,128)S(1)}, u32[]{:S(2)}, u32[]{:S(2)}) collective-permute-start(f32[2,3,128,128]{3,2,1,0:T(8,128)S(1)} %slice.169), channel_id=1, source_target_pairs={{0,8},{1,9},{2,10},{3,11},{4,28},{5,29},{6,30},{7,31},{8,0},{9,1},... | collective-permute-start | bytes 1179656 | tf_op jit(solution)/shard_map/ppermute | solution.py:47
  106.6 0.6 copy-start.12
  115.7 16.9 %collective-permute-start.15 = (f32[4,4,128,128]{3,2,1,0:T(8,128)}, f32[4,4,128,128]{3,2,1,0:T(8,128)S(1)}, u32[]{:S(2)}, u32[]{:S(2)}) collective-permute-start(f32[4,4,128,128]{3,2,1,0:T(8,128)} %get-tuple-element.44), channel_id=1, source_target_pairs={{0,4},{1,5},{2,6},{3,7},{4,0},{5,1},{6,2},{7,3},{8,12},{9,13},{10,... | collective-permute-start | bytes 3145736 | tf_op jit(solution)/shard_map/ppermute | solution.py:47
  115.7 17.5 %collective-permute-start.20 = (f32[4,4,128,128]{3,2,1,0:T(8,128)}, f32[4,4,128,128]{3,2,1,0:T(8,128)S(1)}, u32[]{:S(2)}, u32[]{:S(2)}) collective-permute-start(f32[4,4,128,128]{3,2,1,0:T(8,128)} %get-tuple-element.46), channel_id=1, source_target_pairs={{0,4},{1,5},{2,6},{3,7},{4,0},{5,1},{6,2},{7,3},{8,12},{9,13},{10,... | collective-permute-start | bytes 3145736 | tf_op jit(solution)/shard_map/ppermute | solution.py:47
  117.5 15.1 %copy-start.10 = (f32[4,4,128,128]{3,2,1,0:T(8,128)S(1)}, f32[4,4,128,128]{3,2,1,0:T(8,128)}, u32[]{:S(2)}) copy-start(f32[4,4,128,128]{3,2,1,0:T(8,128)} %get-tuple-element.43) | copy-start | bytes 3145732
  117.5 7.9 %collective-permute-start.7 = (f32[2,3,128,128]{3,2,1,0:T(8,128)S(1)}, f32[2,3,128,128]{3,2,1,0:T(8,128)S(1)}, u32[]{:S(2)}, u32[]{:S(2)}) collective-permute-start(f32[2,3,128,128]{3,2,1,0:T(8,128)S(1)} %slice.163), channel_id=1, source_target_pairs={{0,32},{1,33},{2,34},{3,35},{4,100},{5,101},{6,102},{7,103},{8,40}... | collective-permute-start | bytes 1179656 | tf_op jit(solution)/shard_map/ppermute | solution.py:47
  117.9 10.5 %collective-permute-start.12 = (f32[3,128,128]{2,1,0:T(8,128)S(1)}, f32[3,128,128]{2,1,0:T(8,128)S(1)}, u32[]{:S(2)}, u32[]{:S(2)}) collective-permute-start(f32[3,128,128]{2,1,0:T(8,128)S(1)} %slice_bitcast_fusion.8), channel_id=1, source_target_pairs={{0,24},{1,25},{2,26},{3,27},{4,12},{5,13},{6,14},{7,15},{8,16},{9,... | collective-permute-start | bytes 589832 | tf_op jit(solution)/shard_map/ppermute | solution.py:47
  125.4 7.8 %copy-start.9 = (f32[4,4,128,128]{3,2,1,0:T(8,128)S(1)}, f32[4,4,128,128]{3,2,1,0:T(8,128)}, u32[]{:S(2)}) copy-start(f32[4,4,128,128]{3,2,1,0:T(8,128)} %get-tuple-element.45) | copy-start | bytes 3145732
  125.4 7.1 %collective-permute-start.8 = (f32[3,128,128]{2,1,0:T(8,128)S(1)}, f32[3,128,128]{2,1,0:T(8,128)S(1)}, u32[]{:S(2)}, u32[]{:S(2)}) collective-permute-start(f32[3,128,128]{2,1,0:T(8,128)S(1)} %slice_bitcast_fusion.10), channel_id=1, source_target_pairs={{0,96},{1,97},{2,98},{3,99},{4,36},{5,37},{6,38},{7,39},{8,104},{9... | collective-permute-start | bytes 589832 | tf_op jit(solution)/shard_map/ppermute | solution.py:47
  132.7 9.3 %collective-permute-start.16 = (f32[2,4,128,128]{3,2,1,0:T(8,128)S(1)}, f32[2,4,128,128]{3,2,1,0:T(8,128)S(1)}, u32[]{:S(2)}, u32[]{:S(2)}) collective-permute-start(f32[2,4,128,128]{3,2,1,0:T(8,128)S(1)} %slice_add_fusion.2), channel_id=1, source_target_pairs={{0,8},{1,9},{2,10},{3,11},{4,28},{5,29},{6,30},{7,31},{8,0},{9,1},... | collective-permute-start | bytes 1572872 | tf_op jit(solution)/shard_map/ppermute | solution.py:47
  133.3 11.0 %collective-permute-start.21 = (f32[2,4,128,128]{3,2,1,0:T(8,128)S(1)}, f32[2,4,128,128]{3,2,1,0:T(8,128)S(1)}, u32[]{:S(2)}, u32[]{:S(2)}) collective-permute-start(f32[2,4,128,128]{3,2,1,0:T(8,128)S(1)} %slice_add_fusion), channel_id=1, source_target_pairs={{0,32},{1,33},{2,34},{3,35},{4,100},{5,101},{6,102},{7,103},{8,40}... | collective-permute-start | bytes 1572872 | tf_op jit(solution)/shard_map/ppermute | solution.py:47
  142.1 7.7 %collective-permute-start.17 = (f32[4,128,128]{2,1,0:T(8,128)S(1)}, f32[4,128,128]{2,1,0:T(8,128)S(1)}, u32[]{:S(2)}, u32[]{:S(2)}) collective-permute-start(f32[4,128,128]{2,1,0:T(8,128)S(1)} %slice_bitcast_fusion.6), channel_id=1, source_target_pairs={{0,24},{1,25},{2,26},{3,27},{4,12},{5,13},{6,14},{7,15},{8,16},{9,... | collective-permute-start | bytes 786440 | tf_op jit(solution)/shard_map/ppermute | solution.py:47
  144.4 8.4 %collective-permute-start.22 = (f32[4,128,128]{2,1,0:T(8,128)S(1)}, f32[4,128,128]{2,1,0:T(8,128)S(1)}, u32[]{:S(2)}, u32[]{:S(2)}) collective-permute-start(f32[4,128,128]{2,1,0:T(8,128)S(1)} %slice_bitcast_fusion.4), channel_id=1, source_target_pairs={{0,96},{1,97},{2,98},{3,99},{4,36},{5,37},{6,38},{7,39},{8,104},{9... | collective-permute-start | bytes 786440 | tf_op jit(solution)/shard_map/ppermute | solution.py:47
  147.3 25.7 %collective-permute-start.26 = (f32[2,128,128]{2,1,0:T(8,128)S(1)}, f32[2,128,128]{2,1,0:T(8,128)S(1)}, u32[]{:S(2)}, u32[]{:S(2)}) collective-permute-start(f32[2,128,128]{2,1,0:T(8,128)S(1)} %get-tuple-element.58), channel_id=1, source_target_pairs={{0,5},{1,6},{2,7},{3,4},{4,3},{5,0},{6,1},{7,2},{8,37},{9,38},{10,... | collective-permute-start | bytes 393224 | tf_op jit(solution)/shard_map/ppermute | solution.py:47
  147.4 25.7 %collective-permute-start.27 = (f32[2,128,128]{2,1,0:T(8,128)S(1)}, f32[2,128,128]{2,1,0:T(8,128)S(1)}, u32[]{:S(2)}, u32[]{:S(2)}) collective-permute-start(f32[2,128,128]{2,1,0:T(8,128)S(1)} %get-tuple-element.57), channel_id=1, source_target_pairs={{0,1},{1,2},{2,3},{3,0},{4,7},{5,4},{6,5},{7,6},{8,33},{9,34},{10,... | collective-permute-start | bytes 393224 | tf_op jit(solution)/shard_map/ppermute | solution.py:47
  149.8 28.5 %copy-start.1 = (f32[1,512]{1,0:T(1,128)S(1)}, f32[1,512]{1,0:T(1,128)}, u32[]{:S(2)}) copy-start(f32[1,512]{1,0:T(1,128)} %get-tuple-element.49.near0) | copy-start | bytes 6148
  149.8 28.5 %copy-start.2 = (f32[1,512]{1,0:T(1,128)S(1)}, f32[1,512]{1,0:T(1,128)}, u32[]{:S(2)}) copy-start(f32[1,512]{1,0:T(1,128)} %get-tuple-element.50.near1) | copy-start | bytes 6148
  149.8 28.5 %copy-start.3 = (f32[1,512]{1,0:T(1,128)S(1)}, f32[1,512]{1,0:T(1,128)}, u32[]{:S(2)}) copy-start(f32[1,512]{1,0:T(1,128)} %get-tuple-element.51.far0) | copy-start | bytes 6148
  149.8 6.3 %collective-permute-start.18 = (f32[2,128,128]{2,1,0:T(8,128)S(1)}, f32[2,128,128]{2,1,0:T(8,128)S(1)}, u32[]{:S(2)}, u32[]{:S(2)}) collective-permute-start(f32[2,128,128]{2,1,0:T(8,128)S(1)} %slice.177), channel_id=1, source_target_pairs={{0,32},{1,33},{2,34},{3,35},{4,100},{5,101},{6,102},{7,103},{8,40}... | collective-permute-start | bytes 393224 | tf_op jit(solution)/shard_map/ppermute | solution.py:47
  152.9 8.7 %collective-permute-start.23 = (f32[2,128,128]{2,1,0:T(8,128)S(1)}, f32[2,128,128]{2,1,0:T(8,128)S(1)}, u32[]{:S(2)}, u32[]{:S(2)}) collective-permute-start(f32[2,128,128]{2,1,0:T(8,128)S(1)} %slice.185), channel_id=1, source_target_pairs={{0,8},{1,9},{2,10},{3,11},{4,28},{5,29},{6,30},{7,31},{8,0},{9,1},... | collective-permute-start | bytes 393224 | tf_op jit(solution)/shard_map/ppermute | solution.py:47
  156.1 6.6 %collective-permute-start.19 = (f32[128,128]{1,0:T(8,128)S(1)}, f32[128,128]{1,0:T(8,128)S(1)}, u32[]{:S(2)}, u32[]{:S(2)}) collective-permute-start(f32[128,128]{1,0:T(8,128)S(1)} %slice_bitcast_fusion.16), channel_id=1, source_target_pairs={{0,96},{1,97},{2,98},{3,99},{4,36},{5,37},{6,38},{7,39},{8,104},{9... | collective-permute-start | bytes 196616 | tf_op jit(solution)/shard_map/ppermute | solution.py:47
  161.6 5.6 %collective-permute-start.24 = (f32[128,128]{1,0:T(8,128)S(1)}, f32[128,128]{1,0:T(8,128)S(1)}, u32[]{:S(2)}, u32[]{:S(2)}) collective-permute-start(f32[128,128]{1,0:T(8,128)S(1)} %slice_bitcast_fusion.14), channel_id=1, source_target_pairs={{0,24},{1,25},{2,26},{3,27},{4,12},{5,13},{6,14},{7,15},{8,16},{9,... | collective-permute-start | bytes 196616 | tf_op jit(solution)/shard_map/ppermute | solution.py:47
  167.2 11.0 %collective-permute-start.25 = (f32[4,128,128]{2,1,0:T(8,128)S(1)}, f32[4,128,128]{2,1,0:T(8,128)S(1)}, u32[]{:S(2)}, u32[]{:S(2)}) collective-permute-start(f32[4,128,128]{2,1,0:T(8,128)S(1)} %maximum_select_fusion), channel_id=1, source_target_pairs={{0,4},{1,5},{2,6},{3,7},{4,0},{5,1},{6,2},{7,3},{8,12},{9,13},{10,... | collective-permute-start | bytes 786440 | tf_op jit(solution)/shard_map/ppermute | solution.py:47
  168.2 7.3 %collective-permute-start.28 = (f32[128,128]{1,0:T(8,128)S(1)}, f32[128,128]{1,0:T(8,128)S(1)}, u32[]{:S(2)}, u32[]{:S(2)}) collective-permute-start(f32[128,128]{1,0:T(8,128)S(1)} %get-tuple-element.64), channel_id=1, source_target_pairs={{0,2},{1,3},{2,0},{3,1},{4,6},{5,7},{6,4},{7,5},{8,34},{9,35},{10,... | collective-permute-start | bytes 196616 | tf_op jit(solution)/shard_map/ppermute | solution.py:47
  172.8 5.5 %collective-permute-start.29 = (f32[128,128]{1,0:T(8,128)S(1)}, f32[128,128]{1,0:T(8,128)S(1)}, u32[]{:S(2)}, u32[]{:S(2)}) collective-permute-start(f32[128,128]{1,0:T(8,128)S(1)} %get-tuple-element.63), channel_id=1, source_target_pairs={{0,6},{1,7},{2,4},{3,5},{4,2},{5,3},{6,0},{7,1},{8,38},{9,39},{10,... | collective-permute-start | bytes 196616 | tf_op jit(solution)/shard_map/ppermute | solution.py:47
  179.7 25.4 %collective-permute-start.30 = (f32[128,256]{1,0:T(8,128)S(1)}, f32[128,256]{1,0:T(8,128)S(1)}, u32[]{:S(2)}, u32[]{:S(2)}) collective-permute-start(f32[128,256]{1,0:T(8,128)S(1)} %get-tuple-element.53), channel_id=1, source_target_pairs={{0,32},{1,33},{2,34},{3,35},{4,36},{5,37},{6,38},{7,39},{8,40},{9,... | collective-permute-start | bytes 393224 | tf_op jit(solution)/shard_map/ppermute | solution.py:47
  181.4 23.7 %collective-permute-start.31 = (f32[128,256]{1,0:T(8,128)S(1)}, f32[128,256]{1,0:T(8,128)S(1)}, u32[]{:S(2)}, u32[]{:S(2)}) collective-permute-start(f32[128,256]{1,0:T(8,128)S(1)} %get-tuple-element.54), channel_id=1, source_target_pairs={{0,64},{1,65},{2,66},{3,67},{4,68},{5,69},{6,70},{7,71},{8,72},{9,... | collective-permute-start | bytes 393224 | tf_op jit(solution)/shard_map/ppermute | solution.py:47
  188.9 16.1 %collective-permute-start.32 = (f32[128,256]{1,0:T(8,128)S(1)}, f32[128,256]{1,0:T(8,128)S(1)}, u32[]{:S(2)}, u32[]{:S(2)}) collective-permute-start(f32[128,256]{1,0:T(8,128)S(1)} %get-tuple-element.55), channel_id=1, source_target_pairs={{0,96},{1,97},{2,98},{3,99},{4,100},{5,101},{6,102},{7,103},{8,104... | collective-permute-start | bytes 393224 | tf_op jit(solution)/shard_map/ppermute | solution.py:47
  188.9 16.1 %all-to-all-start.1 = ((f32[128,1,128]{2,1,0:T(1,128)}), f32[128,1,128]{2,1,0:T(1,128)S(1)}, u32[]{:S(2)}, u32[]{:S(2)}) async-start(f32[128,1,128]{2,1,0:T(1,128)} %get-tuple-element.56), calls=%async_computation.1 | async-start | bytes 131072 | tf_op jit(solution)/shard_map/all_to_all | solution.py:383
